TPU v7x, 512 devices: a 4x2x32 block of a 4x8x32 slice. The times are simulated.
512 devices in a mesh: groups: 2 (over y), patch: 128 (over x, z), sub: 2 (over core).
Axes of the slice: x: 4, y: 2, z: 32, core: 2. Of those that a mesh axis runs over, the one named last changes fastest.
The devices are a block of a 4x8x32 slice.
Arguments:
- block_cols: int32 [1024, 3], P(('groups', 'patch', 'sub')), parts along dimension 0, may hold values from 0 to 511, as said below
- step_tiles: float32 [1024, 3, 128, 128], P(('groups', 'patch', 'sub')), parts along dimension 0, as said below
- mass: float32 [131072], P(('groups', 'patch', 'sub')), parts along dimension 0, as said below
- warm_start: float32 [131072, 128], P(('groups', 'patch', 'sub')), parts along dimension 0, may hold values from -2.5 to 2.5
- source_ids: int32 [256], P('groups'), parts along dimension 0, may hold values from 0 to 65535
Outputs:
- solution: float32 [131072, 128], P(('groups', 'patch', 'sub')), parts along dimension 0
There are 2 independent parts, one for each index of `groups`. A program takes and returns all parts, laid end to end along the dimension named above; each array names one. Nothing has to cross between parts.
Inputs may be any that keep to these rules, and one draw needn't show every extreme that they name: `block_cols`: slot lists of block row g name g itself and blocks within 1 of g coupled to it; coupling is symmetric (g names h exactly when h names g). Unused slots name g and carry a zero tile. `step_tiles`: entries are not negative. The tile of block row h toward g is the transpose of the tile of row g toward h; the tile of a row toward itself is symmetric with a zero diagonal. `mass`: between 0.1 and 1.2.
All inputs are finite; a program needn't handle non-finite values.
Results may differ from a plain program's by a relative error of at most 0.00023.
Values sent between devices are 32-bit elements; how exact they have to be, the bound alone decides.
A program may use at most 64 MiB of HBM per device.

v0:
```python
import functools

import jax
import jax.numpy as jnp
from jax import lax
from jax.sharding import Mesh
from jax.sharding import PartitionSpec as P

REACH = 1
ITERS = 2
PATCH_SUB = ("patch_0", "patch_1", "sub")
GROUPS_PATCH_SUB = ("groups", "patch_0", "patch_1", "sub")


def by_axis(shard, axes):
    return functools.reduce(lax.psum, axes, shard)


def extended_2(shard, sides, width):
    edges = {}
    for axis, dim in sides:
        size, length = (lax.axis_size(axis), shard.shape[dim])
        up = [(i, (i + 1) % size) for i in range(size - 1)]
        last = lax.slice_in_dim(shard, length - width, length, axis=dim)
        leading = lax.slice_in_dim(shard, 0, width, axis=dim)
        edges[dim] = (
            lax.ppermute(last, axis, up),
            lax.ppermute(leading, axis, [(b, a) for a, b in up]),
        )
    done = []
    for _, dim in sides:
        low, high = edges[dim]
        around = [(width, width) if d in done else (0, 0) for d in range(shard.ndim)]
        shard = jnp.concatenate([jnp.pad(low, around), shard, jnp.pad(high, around)], axis=dim)
        done.append(dim)
    return shard


def apply_operator(operand, extend, local_cols, step_tiles, diag_total):
    tile_size = step_tiles.shape[-1]
    extended = extend(operand)
    blocks = extended.reshape(-1, tile_size, operand.shape[1])
    picked = blocks[local_cols]
    coupled = jnp.einsum(
        "bkij,bkjs->bis",
        step_tiles,
        picked,
        precision=lax.Precision.HIGHEST,
        preferred_element_type=jnp.float32,
    )
    return diag_total * operand - coupled.reshape(operand.shape)


def paired_products(residual, image_vec):
    return (
        by_axis(jnp.sum(residual * residual, axis=0), PATCH_SUB),
        by_axis(jnp.sum(residual * image_vec, axis=0), PATCH_SUB),
    )


def body(block_cols, step_tiles, mass, warm_start, source_ids):
    blocks_here = block_cols.shape[0]
    tile_size = step_tiles.shape[-1]
    rim_rows = REACH * tile_size
    rows_here = blocks_here * tile_size
    position = lax.axis_index(PATCH_SUB)
    local_cols = block_cols - (position * blocks_here - REACH)
    degree = jnp.sum(step_tiles, axis=(1, 3)).reshape(rows_here)
    diag_total = (mass + degree)[:, None]
    vertex_ids = position * rows_here + jnp.arange(rows_here, dtype=jnp.int32)
    rhs = (vertex_ids[:, None] == source_ids[None, :]).astype(jnp.float32)

    def extend(operand):
        return extended_2(operand, ((PATCH_SUB, 0),), rim_rows)

    def operator(operand):
        return apply_operator(operand, extend, local_cols, step_tiles, diag_total)

    solution = warm_start
    residual = rhs - operator(warm_start)
    image_vec = operator(residual)
    norm_now, product = paired_products(residual, image_vec)
    alpha_step = norm_now / product
    direction = residual
    along = image_vec
    for iteration in range(ITERS):
        solution = solution + alpha_step * direction
        residual = residual - alpha_step * along
        if iteration + 1 < ITERS:
            image_vec = operator(residual)
            norm_next, product = paired_products(residual, image_vec)
            ratio = norm_next / norm_now
            alpha_step = norm_next / (product - ratio * norm_next / alpha_step)
            direction = residual + ratio * direction
            along = image_vec + ratio * along
            norm_now = norm_next
    return solution


def solution(mesh):
    split = Mesh(
        mesh.devices.reshape(mesh.shape["groups"], 4, 32, mesh.shape["sub"]),
        ("groups", "patch_0", "patch_1", "sub"),
    )
    placed = (
        P(GROUPS_PATCH_SUB, None),
        P(GROUPS_PATCH_SUB, None, None, None),
        P(GROUPS_PATCH_SUB),
        P(GROUPS_PATCH_SUB, None),
        P("groups"),
    )
    return jax.shard_map(
        body, mesh=split, in_specs=placed, out_specs=P(GROUPS_PATCH_SUB, None), check_vma=False
    )
```

profile of v0, /device:TPU:40, one launch (start us, length us, event | category | flops | bytes accessed | tf_op | source)
XLA Modules:
  0.0 203.5 jit_solution(7948396330499817289)
XLA Ops:
  0.0 0.9 fusion.5
  0.9 1.8 collective-permute-start
  2.7 1.3 collective-permute-start.1
  4.1 0.7 copy-done.3
  4.8 1.1 reduce_sum.45
  6.0 2.4 %collective-permute-done.1 = f32[128,128]{1,0:T(8,128)S(1)} collective-permute-done((f32[128,128]{1,0:T(8,128)S(1)}, f32[128,128]{1,0:T(8,128)S(1)}, u32[]{:S(2)}, u32[]{:S(2)}) %collective-permute-start.1) | collective-permute-done | bytes 65568 | tf_op jit(solution)/shard_map/ppermute | solution.py:28
  8.4 0.6 gather_fusion
  10.2 4.9 %collective-permute-start.2 = (f32[128,128]{1,0:T(8,128)S(1)}, f32[128,128]{1,0:T(8,128)S(1)}, u32[]{:S(2)}, u32[]{:S(2)}) collective-permute-start(f32[128,128]{1,0:T(8,128)S(1)} %get-tuple-element.25), channel_id=1, source_target_pairs={{0,1},{1,2},{2,3},{3,4},{4,5},{5,6},{6,7},{7,8},{8,9},{9,10},{10,1... | collective-permute-start | bytes 196616 | tf_op jit(solution)/shard_map/ppermute | solution.py:27
  15.1 1.3 collective-permute-start.3
  16.4 1.9 collective-permute-done.3
  18.3 0.6 gather_fusion.1
  18.9 0.5 fusion.7
  19.5 53.9 %all-reduce.3 = (f32[128]{0:T(128)S(1)}, f32[128]{0:T(128)S(1)}) all-reduce(f32[128]{0:T(128)S(1)} %get-tuple-element.8, f32[128]{0:T(128)S(1)} %get-tuple-element.7), channel_id=1, replica_groups=mesh['groups'=2,'patch_0'=4,'patch_1'=32,'sub'=2] {'patch_0'}, use_global_device_ids=true, to_apply=%region_2.3 | all-reduce | flops 256 | bytes 2048 | tf_op jit(solution)/shard_map/psum | solution.py:16
  73.5 52.8 %all-reduce.1 = (f32[128]{0:T(128)S(1)}, f32[128]{0:T(128)S(1)}) all-reduce(f32[128]{0:T(128)S(1)} %get-tuple-element.15, f32[128]{0:T(128)S(1)} %get-tuple-element.16), channel_id=1, replica_groups=mesh['groups'=2,'patch_0'=4,'patch_1'=32,'sub'=2] {'patch_1'}, use_global_device_ids=true, to_apply=%region_3.4 | all-reduce | flops 256 | bytes 2048 | tf_op jit(solution)/shard_map/psum | solution.py:16
  126.3 2.5 %all-reduce.5 = (f32[128]{0:T(128)S(1)}, f32[128]{0:T(128)S(1)}) all-reduce(f32[128]{0:T(128)S(1)} %get-tuple-element.11, f32[128]{0:T(128)S(1)} %get-tuple-element.12), channel_id=1, replica_groups=mesh['groups'=2,'patch_0'=4,'patch_1'=32,'sub'=2] {'sub'}, use_global_device_ids=true, to_apply=%region_4.5 | all-reduce | flops 256 | bytes 2048 | tf_op jit(solution)/shard_map/psum | solution.py:16
  128.9 2.1 %collective-permute-start.4 = (f32[128,128]{1,0:T(8,128)S(1)}, f32[128,128]{1,0:T(8,128)S(1)}, u32[]{:S(2)}, u32[]{:S(2)}) collective-permute-start(f32[128,128]{1,0:T(8,128)S(1)} %get-tuple-element.23), channel_id=1, source_target_pairs={{0,1},{1,2},{2,3},{3,4},{4,5},{5,6},{6,7},{7,8},{8,9},{9,10},{10,1... | collective-permute-start | bytes 196616 | tf_op jit(solution)/shard_map/ppermute | solution.py:27
  131.1 1.3 collective-permute-start.5
  132.4 3.3 %collective-permute-done.5 = f32[128,128]{1,0:T(8,128)S(1)} collective-permute-done((f32[128,128]{1,0:T(8,128)S(1)}, f32[128,128]{1,0:T(8,128)S(1)}, u32[]{:S(2)}, u32[]{:S(2)}) %collective-permute-start.5) | collective-permute-done | bytes 65568 | tf_op jit(solution)/shard_map/ppermute | solution.py:28
  135.7 0.6 gather_fusion.2
  136.3 0.5 fusion.8
  136.9 10.5 %all-reduce.2 = (f32[128]{0:T(128)S(1)}, f32[128]{0:T(128)S(1)}) all-reduce(f32[128]{0:T(128)S(1)} %get-tuple-element.6, f32[128]{0:T(128)S(1)} %get-tuple-element.5), channel_id=1, replica_groups=mesh['groups'=2,'patch_0'=4,'patch_1'=32,'sub'=2] {'patch_0'}, use_global_device_ids=true, to_apply=%region_10.11 | all-reduce | flops 256 | bytes 2048 | tf_op jit(solution)/shard_map/psum | solution.py:16
  147.4 52.9 %all-reduce = (f32[128]{0:T(128)S(1)}, f32[128]{0:T(128)S(1)}) all-reduce(f32[128]{0:T(128)S(1)} %get-tuple-element.13, f32[128]{0:T(128)S(1)} %get-tuple-element.14), channel_id=1, replica_groups=mesh['groups'=2,'patch_0'=4,'patch_1'=32,'sub'=2] {'patch_1'}, use_global_device_ids=true, to_apply=%region_11.12 | all-reduce | flops 256 | bytes 2048 | tf_op jit(solution)/shard_map/psum | solution.py:16
  200.3 2.5 %all-reduce.4 = (f32[128]{0:T(128)S(1)}, f32[128]{0:T(128)S(1)}) all-reduce(f32[128]{0:T(128)S(1)} %get-tuple-element.9, f32[128]{0:T(128)S(1)} %get-tuple-element.10), channel_id=1, replica_groups=mesh['groups'=2,'patch_0'=4,'patch_1'=32,'sub'=2] {'sub'}, use_global_device_ids=true, to_apply=%region_12.13 | all-reduce | flops 256 | bytes 2048 | tf_op jit(solution)/shard_map/psum | solution.py:16
  202.8 0.7 multiply_add_fusion
  (29 shorter events, 1.8 us)
Async XLA Ops:
  0.9 5.2 %collective-permute-start = (f32[128,128]{1,0:T(8,128)S(1)}, f32[128,128]{1,0:T(8,128)S(1)}, u32[]{:S(2)}, u32[]{:S(2)}) collective-permute-start(f32[128,128]{1,0:T(8,128)S(1)} %get-tuple-element.27), channel_id=1, source_target_pairs={{0,1},{1,2},{2,3},{3,4},{4,5},{5,6},{6,7},{7,8},{8,9},{9,10},{10,1... | collective-permute-start | bytes 196616 | tf_op jit(solution)/shard_map/ppermute | solution.py:27
  2.7 5.7 %collective-permute-start.1 = (f32[128,128]{1,0:T(8,128)S(1)}, f32[128,128]{1,0:T(8,128)S(1)}, u32[]{:S(2)}, u32[]{:S(2)}) collective-permute-start(f32[128,128]{1,0:T(8,128)S(1)} %get-tuple-element.28), channel_id=1, source_target_pairs={{1,0},{2,1},{3,2},{4,3},{5,4},{6,5},{7,6},{8,7},{9,8},{10,9},{11,1... | collective-permute-start | bytes 196616 | tf_op jit(solution)/shard_map/ppermute | solution.py:28
  4.1 0.7 copy-start.3
  4.8 1.2 copy-start.2
  4.8 3.6 %copy-start.1 = (f32[256,128]{1,0:T(8,128)S(1)}, f32[256,128]{1,0:T(8,128)}, u32[]{:S(2)}) copy-start(f32[256,128]{1,0:T(8,128)} %param.8) | copy-start | bytes 393220
  8.4 1.0 copy-start
  9.4 0.7 copy-start.4
  10.2 6.2 %collective-permute-start.2 = (f32[128,128]{1,0:T(8,128)S(1)}, f32[128,128]{1,0:T(8,128)S(1)}, u32[]{:S(2)}, u32[]{:S(2)}) collective-permute-start(f32[128,128]{1,0:T(8,128)S(1)} %get-tuple-element.25), channel_id=1, source_target_pairs={{0,1},{1,2},{2,3},{3,4},{4,5},{5,6},{6,7},{7,8},{8,9},{9,10},{10,1... | collective-permute-start | bytes 196616 | tf_op jit(solution)/shard_map/ppermute | solution.py:27
  15.1 3.2 %collective-permute-start.3 = (f32[128,128]{1,0:T(8,128)S(1)}, f32[128,128]{1,0:T(8,128)S(1)}, u32[]{:S(2)}, u32[]{:S(2)}) collective-permute-start(f32[128,128]{1,0:T(8,128)S(1)} %get-tuple-element.26), channel_id=1, source_target_pairs={{1,0},{2,1},{3,2},{4,3},{5,4},{6,5},{7,6},{8,7},{9,8},{10,9},{11,1... | collective-permute-start | bytes 196616 | tf_op jit(solution)/shard_map/ppermute | solution.py:28
  128.9 3.4 %collective-permute-start.4 = (f32[128,128]{1,0:T(8,128)S(1)}, f32[128,128]{1,0:T(8,128)S(1)}, u32[]{:S(2)}, u32[]{:S(2)}) collective-permute-start(f32[128,128]{1,0:T(8,128)S(1)} %get-tuple-element.23), channel_id=1, source_target_pairs={{0,1},{1,2},{2,3},{3,4},{4,5},{5,6},{6,7},{7,8},{8,9},{9,10},{10,1... | collective-permute-start | bytes 196616 | tf_op jit(solution)/shard_map/ppermute | solution.py:27
  131.1 4.6 %collective-permute-start.5 = (f32[128,128]{1,0:T(8,128)S(1)}, f32[128,128]{1,0:T(8,128)S(1)}, u32[]{:S(2)}, u32[]{:S(2)}) collective-permute-start(f32[128,128]{1,0:T(8,128)S(1)} %get-tuple-element.24), channel_id=1, source_target_pairs={{1,0},{2,1},{3,2},{4,3},{5,4},{6,5},{7,6},{8,7},{9,8},{10,9},{11,1... | collective-permute-start | bytes 196616 | tf_op jit(solution)/shard_map/ppermute | solution.py:28
where the time goes:
time: 205 us; the launch traced here: 204 us
  blocking collectives  175 us (85%)
  starting transfers between devices  12.7 us (6%)
  waiting for transfers between devices  7.5 us (4%)
  local copies, waits for them, and re-layouts  3.94 us (2%)
  other arithmetic  2.43 us (1%)
    psum x6, blocking collectives, by_axis(): return functools.reduce(lax.psum, axes, shard)  175 us
    ppermute x3, starting transfers between devices, extended_2(): lax.ppermute(last, axis, up)  8.82 us
    ppermute x3, waiting for transfers between devices, extended_2(): lax.ppermute(leading, axis, [(b, a) for a, b in up])  7.5 us
  transfers between devices with their start and end apart: 6, of which 3 were waited for; matrix products, arithmetic and copies ran while one was open for 1% of the time, Pallas kernels for 0%

commit v1 on v0

v1 whole, which is shorter than its diff:
```python
import functools

import jax
import jax.numpy as jnp
from jax import lax
from jax.experimental import pallas as pl
from jax.experimental.pallas import tpu as pltpu
from jax.sharding import Mesh
from jax.sharding import PartitionSpec as P

NZ = 32
AXES = ("groups", "patch_0", "patch_1", "sub")
MESH = pl.DeviceIdType.MESH
F32, BF16 = jnp.float32, jnp.bfloat16
ANY = pl.BlockSpec(memory_space=pl.ANY)
VMEM = pl.BlockSpec(memory_space=pltpu.VMEM)


def halves(value):
    high = value.astype(BF16)
    return high, (value - high.astype(F32)).astype(BF16)


def pair(value):
    return jnp.concatenate(halves(value), axis=1)


def product(high, low, packed):
    n = packed.shape[1] // 2
    both = jnp.dot(high, packed, preferred_element_type=F32) + jnp.dot(low, packed, preferred_element_type=F32)
    return both[:, :n] + both[:, n:]


def rows_sum(value):
    return jnp.sum(value, axis=0, keepdims=True)


def merged(buf):
    sq, cross, about, rss, quad, lin = (buf[:, k, :] for k in range(6))
    sq_all, cross_all = rows_sum(sq), rows_sum(cross)
    centre = jnp.where(sq_all > 0, cross_all / sq_all, 0.0)
    off = about - centre
    first = cross - about * sq
    rss_all = rows_sum(rss + off * (2.0 * first + off * sq))
    quad_all = rows_sum(quad + off * (lin + off * cross))
    lin_all = rows_sum(lin + 2.0 * off * cross)
    return sq_all, cross_all, centre, rss_all, quad_all, lin_all


def kernel(
    nx, tile,
    cols_h, tiles_h, mass_h, x_h, src_h,
    r_o, w_o, co_o,
    cols, tiles, mass, x, src,
    halo_x, halo_s, halo_w, s_buf, w_buf, own, plane, ranks, plane_sum, total,
    in_sem, x_ss, x_rs, s_ss, s_rs, w_ss, w_rs, p_ss, p_rs, z_ss, z_rs, b_ss, b_rs,
):
    g, px, pz, pc = (lax.axis_index(name) for name in AXES)
    bar = pltpu.get_barrier_semaphore()

    def turn_x(d):
        return lax.rem(px + d + nx, nx)

    def turn_z(d):
        return lax.rem(pz + d + NZ, NZ)

    first, last = pz == 0, pz == NZ - 1
    right = (
        g,
        jnp.where((pc == 1) & last, turn_x(1), px),
        jnp.where(pc == 1, turn_z(1), pz),
        1 - pc,
    )
    left = (
        g,
        jnp.where((pc == 0) & first, turn_x(-1), px),
        jnp.where(pc == 0, turn_z(-1), pz),
        1 - pc,
    )
    far = tuple(jnp.where(pc == 1, a, b) for a, b in zip(right, left))

    def greet(x_at, z_at, c_at):
        pl.semaphore_signal(bar, inc=1, device_id=(g, x_at, z_at, c_at), device_id_type=MESH)

    greet(*far[1:])
    greet(px, pz, 1 - pc)
    for d in range(1, nx):
        for c in range(2):
            greet(turn_x(d), pz, c)

    @pl.when(pc == 1)
    def _():
        greet(px, turn_z(1), pc)
        greet(px, turn_z(-1), pc)

    @pl.when((pc == 1) & first)
    def _():
        for k in range(1, NZ):
            greet(px, k, pc)

    loads = [
        pltpu.make_async_copy(a, b, in_sem.at[i])
        for i, (a, b) in enumerate(((x_h, x), (tiles_h, tiles), (mass_h, mass), (src_h, src), (cols_h, cols)))
    ]
    for load in loads:
        load.start()
    pl.semaphore_wait(bar, 2 * nx + jnp.where(pc == 1, jnp.where(first, 2, 3), 0))

    def send(ref_lo, ref_hi, slots, ss, rs):
        out = [
            pltpu.make_async_remote_copy(ref_hi, slots.at[0], ss.at[0], rs.at[0], device_id=right, device_id_type=MESH),
            pltpu.make_async_remote_copy(ref_lo, slots.at[1], ss.at[1], rs.at[1], device_id=left, device_id_type=MESH),
        ]
        for copy in out:
            copy.start()
        return out

    loads[0].wait()
    sent_x = send(x.at[pl.ds(0, tile)], x.at[pl.ds(tile, tile)], halo_x, x_ss, x_rs)
    for load in loads[1:]:
        load.wait()

    position = (px * NZ + pz) * 2 + pc
    parts = []
    for b in range(2):
        here = position * 2 + b
        found = []
        for d in (-1, 0, 1):
            found.append(sum((cols[b, k] == here + d).astype(F32) * tiles[b, k] for k in range(3)))
        parts.append(found)
    (t0l, t00, t01), (t10, t11, t1r) = parts
    eye = lax.broadcasted_iota(jnp.int32, (tile, tile), 0) == lax.broadcasted_iota(jnp.int32, (tile, tile), 1)
    ones = jnp.ones((tile, tile), BF16)
    diag = []
    for b in range(2):
        row = mass[pl.ds(b * tile, tile)].reshape(1, tile)
        rest = jnp.where(eye, row, 0.0) + (parts[b][0] + parts[b][1] + parts[b][2])
        high = rest.astype(BF16)
        rest = rest - high.astype(F32)
        mid = rest.astype(BF16)
        low = (rest - mid.astype(F32)).astype(BF16)
        diag.append(sum(jnp.dot(part, ones, preferred_element_type=F32) for part in (low, mid, high)))
    diag = jnp.concatenate(diag, axis=0)
    inner = halves(jnp.concatenate([jnp.concatenate([t00, t01], axis=1), jnp.concatenate([t10, t11], axis=1)], axis=0))
    to_left, to_right = halves(t0l), halves(t1r)

    x_pair = pair(x[...])
    ids = lax.broadcasted_iota(jnp.int32, (2 * tile, src.shape[0]), 0) + position * 2 * tile
    rhs = (ids == src[...].reshape(1, -1)).astype(F32)
    s = rhs - diag * x[...] + product(*inner, x_pair)
    s_buf[...] = s
    from_left, from_right = halves(t0l.T), halves(t1r.T)
    sent_s = send(s_buf.at[pl.ds(0, tile)], s_buf.at[pl.ds(tile, tile)], halo_s, s_ss, s_rs)
    on_left = product(*from_left, x_pair[:tile])
    on_right = product(*from_right, x_pair[tile:])

    for copy in sent_x:
        copy.wait()
    r = s + jnp.concatenate([product(*to_left, pair(halo_x[0])), product(*to_right, pair(halo_x[1]))], axis=0)
    r_o[...] = r
    near = diag * r - product(*inner, pair(r))
    for copy in sent_s:
        copy.wait()
    w = near - jnp.concatenate(
        [product(*to_left, pair(halo_s[0] + on_left)), product(*to_right, pair(halo_s[1] + on_right))], axis=0
    )
    w_buf[...] = w
    w_o[...] = w
    sent_w = send(w_buf.at[pl.ds(0, tile)], w_buf.at[pl.ds(tile, tile)], halo_w, w_ss, w_rs)

    sq, cross = rows_sum(r * r), rows_sum(r * w)
    ceiling = 2.0 * jnp.max(diag)
    about = jnp.where(sq > 0, jnp.clip(cross / sq, 0.0, ceiling), 0.0)
    u = w - about * r
    rss = rows_sum(u * u)
    v_near = diag * w - product(*inner, pair(w))
    for copy in sent_w:
        copy.wait()
    v = v_near - jnp.concatenate([product(*to_left, pair(halo_w[0])), product(*to_right, pair(halo_w[1]))], axis=0)
    y = v - about * w
    quad, lin = rows_sum(u * y), rows_sum(u * w + r * y)
    blank = jnp.zeros((2, sq.shape[1]), F32)
    mine = jnp.concatenate([sq, cross, about, rss, quad, lin, blank], axis=0)
    own[...] = mine

    slot = px * 2 + pc
    to_plane = [
        pltpu.make_async_remote_copy(
            own, plane.at[slot], p_ss.at[d], p_rs.at[slot], device_id=(g, turn_x(d), pz, 1), device_id_type=MESH
        )
        for d in range(nx)
    ]
    for copy in to_plane[1:]:
        copy.start()

    @pl.when(pc == 0)
    def _():
        to_plane[0].start()

    down = pltpu.make_async_remote_copy(
        plane_sum, ranks.at[pz], z_ss, z_rs.at[pz], device_id=(g, px, 0, 1), device_id_type=MESH
    )

    def pass_on(c, z_at, k):
        return pltpu.make_async_remote_copy(
            total, total, b_ss.at[k], b_rs, device_id=(g, px, z_at, c), device_id_type=MESH
        )

    half = NZ // 2
    across, up, back = pass_on(0, pz, 0), pass_on(1, turn_z(1), 1), pass_on(1, turn_z(-1), 2)

    @pl.when(pc == 1)
    def _():
        plane[slot] = mine
        for d in range(nx):
            for c in range(2):
                if (d, c) != (0, 1):
                    at = turn_x(d) * 2 + c
                    pltpu.make_async_copy(plane.at[at], plane.at[at], p_rs.at[at]).wait()
        rows = merged(plane)
        joined = jnp.concatenate([*rows, blank], axis=0)

        @pl.when(first)
        def _():
            ranks[0] = joined
            for k in range(1, NZ):
                pltpu.make_async_copy(ranks.at[k], ranks.at[k], z_rs.at[k]).wait()
            sq, cross, _, rss, quad, _ = merged(ranks)
            step = sq / cross
            after = step * step * rss
            ratio = after / sq
            step_next = after / (step * step * quad - ratio * after / step)
            total[...] = jnp.concatenate(
                [step + step_next * (1.0 + ratio), -(step_next * step), jnp.zeros((6, sq.shape[1]), F32)], axis=0
            )

        @pl.when(jnp.logical_not(first))
        def _():
            plane_sum[...] = joined
            down.start()
            pltpu.make_async_copy(total, total, b_rs).wait()

        @pl.when(pz < half)
        def _():
            up.start()

        @pl.when(first | (pz > half + 1))
        def _():
            back.start()

        across.start()

    @pl.when(pc == 0)
    def _():
        pltpu.make_async_copy(total, total, b_rs).wait()

    co_o[...] = total[...]

    for copy in to_plane[1:]:
        copy.wait_send()

    @pl.when(pc == 0)
    def _():
        to_plane[0].wait_send()

    @pl.when(pc == 1)
    def _():
        @pl.when(jnp.logical_not(first))
        def _():
            down.wait_send()

        @pl.when(pz < half)
        def _():
            up.wait_send()

        @pl.when(first | (pz > half + 1))
        def _():
            back.wait_send()

        across.wait_send()


def body(block_cols, step_tiles, mass, warm_start, source_ids):
    nx = lax.axis_size("patch_0")
    tile = step_tiles.shape[-1]
    rows, width = warm_start.shape
    block = (2, tile, width)
    sem = pltpu.SemaphoreType.DMA
    r, w, co = pl.pallas_call(
        functools.partial(kernel, nx, tile),
        out_shape=[
            jax.ShapeDtypeStruct((rows, width), F32),
            jax.ShapeDtypeStruct((rows, width), F32),
            jax.ShapeDtypeStruct((8, width), F32),
        ],
        in_specs=[ANY] * 5,
        out_specs=[VMEM] * 3,
        scratch_shapes=[
            pltpu.SMEM(block_cols.shape, jnp.int32),
            pltpu.VMEM(step_tiles.shape, F32),
            pltpu.VMEM(mass.shape, F32),
            pltpu.VMEM((rows, width), F32),
            pltpu.VMEM(source_ids.shape, jnp.int32),
            pltpu.VMEM(block, F32),
            pltpu.VMEM(block, F32),
            pltpu.VMEM(block, F32),
            pltpu.VMEM((rows, width), F32),
            pltpu.VMEM((rows, width), F32),
            pltpu.VMEM((8, width), F32),
            pltpu.VMEM((2 * nx, 8, width), F32),
            pltpu.VMEM((NZ, 8, width), F32),
            pltpu.VMEM((8, width), F32),
            pltpu.VMEM((8, width), F32),
            sem((5,)),
            sem((2,)), sem((2,)),
            sem((2,)), sem((2,)),
            sem((2,)), sem((2,)),
            sem((nx,)), sem((2 * nx,)),
            sem, sem((NZ,)),
            sem((3,)), sem,
        ],
        compiler_params=pltpu.CompilerParams(collective_id=0, has_side_effects=True),
        name="heat",
    )(block_cols, step_tiles, mass, warm_start, source_ids)
    return warm_start + co[0:1] * r + co[1:2] * w


def solution(mesh):
    split = Mesh(
        mesh.devices.reshape(mesh.shape["groups"], mesh.shape["patch"] // NZ, NZ, mesh.shape["sub"]), AXES
    )
    placed = (P(AXES, None), P(AXES, None, None, None), P(AXES), P(AXES, None), P("groups"))
    return jax.shard_map(body, mesh=split, in_specs=placed, out_specs=P(AXES, None), check_vma=False)
```

time: 205 us -> 66.5 us (0.32)
  blocking collectives: 175 us -> 0 us
  Pallas kernels: 0 us -> 62.8 us
  starting transfers between devices: 12.7 us -> 0 us
  waiting for transfers between devices: 7.5 us -> 0 us
  local copies, waits for them, and re-layouts: 3.94 us -> 0.76 us
    psum x6 -> x0, blocking collectives: 175 us -> none  [by_axis(): return functools.reduce(lax.psum, axes, shard)]
    pallas_call x0 -> x1, Pallas kernels: none -> 62.8 us  [body(): pl.pallas_call(functools.partial(kernel, nx, tile), out_shape=[jax.ShapeD...]
    ppermute x6 -> x0, starting transfers between devices: 12.7 us -> none  [the longest x3 8.82 us: extended_2(): lax.ppermute(last, axis, up)]
    ppermute x6 -> x0, waiting for transfers between devices: 7.5 us -> none  [the longest x3 7.5 us: extended_2(): lax.ppermute(leading, axis, [(b, a) for a, b in up])]
  transfers between devices with their start and end apart: 6 -> 0, of which waited for: 3 -> 0; matrix products, arithmetic and copies ran while one was open for 1% -> 0% of each run, Pallas kernels for 0% -> 0%
where the time goes in v1:
time: 66.5 us; the launch traced here: 65.2 us
  Pallas kernels  62.8 us (94%)
  other arithmetic  1.64 us (2%)
  local copies, waits for them, and re-layouts  0.76 us (1%)
    pallas_call x1, Pallas kernels, body(): pl.pallas_call(functools.partial(kernel, nx, tile), out_shape=[jax.ShapeD...  62.8 us
    add x1, other arithmetic, body(): return warm_start + co[0:1] * r + co[1:2] * w  1.64 us

profile of v1, /device:TPU:40, one launch (start us, length us, event | category | flops | bytes accessed | tf_op | source)
XLA Modules:
  0.0 65.2 jit_solution(2260217696227038754)
XLA Ops:
  0.0 0.0 copy-start
  0.0 62.8 %heat.1 = (f32[256,128]{1,0:T(8,128)}, f32[256,128]{1,0:T(8,128)}, f32[8,128]{1,0:T(8,128)}) custom-call(s32[2,3]{1,0:T(2,128)} %cols_h.1, f32[2,3,128,128]{3,2,1,0:T(8,128)} %tiles_h.1, f32[256]{0:T(256)} %mass_h.1, f32[256,128]{1,0:T(8,128)} %x_h.1, s32[128]{0:T(128)} %src_h.1), custom_call_target="tpu_custom_call" | custom-call | tf_op jit(solution)/shard_map/heat/pallas_call | solution.py:289
  62.8 0.8 %slice_bitcast_fusion.1 = (f32[128]{0:T(128)S(1)}, f32[128]{0:T(128)S(1)}) fusion(f32[8,128]{1,0:T(8,128)} %get-tuple-element.8), kind=kLoop, calls=%fused_computation.2 | loop fusion | bytes 2048 | tf_op jit(solution)/shard_map/mul | solution.py:325
  63.6 0.0 copy-done
  63.6 1.6 %multiply_add_fusion = f32[256,128]{1,0:T(8,128)} fusion(f32[256,128]{1,0:T(8,128)} %get-tuple-element.10, f32[256,128]{1,0:T(8,128)S(1)} %copy-done, f32[256,128]{1,0:T(8,128)} %get-tuple-element.9, f32[128]{0:T(128)S(1)} %get-tuple-element.12, f32[128]{0:T(128)S(1)} %get-tuple-element.11), kind=kLoop, calls=%fused_computation | loop fusion | flops 131072 | bytes 525312 | tf_op jit(solution)/shard_map/add | solution.py:325
Async XLA Ops:
  0.0 63.6 %copy-start = (f32[256,128]{1,0:T(8,128)S(1)}, f32[256,128]{1,0:T(8,128)}, u32[]{:S(2)}) copy-start(f32[256,128]{1,0:T(8,128)} %x_h.1) | copy-start | bytes 393220

commit v2 on v1

v2 whole, which is shorter than its diff:
```python
import functools

import jax
import jax.numpy as jnp
from jax import lax
from jax.experimental import pallas as pl
from jax.experimental.pallas import tpu as pltpu
from jax.sharding import Mesh
from jax.sharding import PartitionSpec as P

NZ = 32
DIRECT = 3
AXES = ("groups", "patch_0", "patch_1", "sub")
MESH = pl.DeviceIdType.MESH
F32, BF16 = jnp.float32, jnp.bfloat16
ANY = pl.BlockSpec(memory_space=pl.ANY)


def halves(value):
    high = value.astype(BF16)
    return high, (value - high.astype(F32)).astype(BF16)


def pair(value):
    return jnp.concatenate(halves(value), axis=1)


def product(high, low, packed):
    n = packed.shape[1] // 2
    both = jnp.dot(high, packed, preferred_element_type=F32) + jnp.dot(low, packed, preferred_element_type=F32)
    return both[:, :n] + both[:, n:]


def rows_sum(value):
    return jnp.sum(value, axis=0, keepdims=True)


def merged(buf):
    sq, cross, about, rss, quad, lin, curv = (buf[:, k, :] for k in range(7))
    sq_all, cross_all = rows_sum(sq), rows_sum(cross)
    centre = jnp.where(sq_all > 0, cross_all / sq_all, 0.0)
    off = about - centre
    first = cross - about * sq
    rss_all = rows_sum(rss + off * (2.0 * first + off * sq))
    quad_all = rows_sum(quad + off * (lin + off * curv))
    lin_all = rows_sum(lin + 2.0 * off * curv)
    return sq_all, cross_all, centre, rss_all, quad_all, lin_all, rows_sum(curv)


def kernel(
    nx, tile,
    cols_h, tiles_h, mass_h, x_h, src_h,
    out,
    cols, tiles, mass, x, src,
    halo_x, halo_s, halo_w, halo_m, halo_q, s_buf, w_buf, m_buf, q_buf, own, ranks, plane_sum, total,
    in_sem, x_ss, x_rs, s_ss, s_rs, w_ss, w_rs, m_ss, m_rs, q_ss, q_rs, p_ss, z_ss, z_rs, b_ss, b_rs,
):
    g, px, pz, pc = (lax.axis_index(name) for name in AXES)
    bar = pltpu.get_barrier_semaphore()

    def turn_x(d):
        return lax.rem(px + d + nx, nx)

    def turn_z(d):
        return lax.rem(pz + d + NZ, NZ)

    first, last = pz == 0, pz == NZ - 1
    right = (
        g,
        jnp.where((pc == 1) & last, turn_x(1), px),
        jnp.where(pc == 1, turn_z(1), pz),
        1 - pc,
    )
    left = (
        g,
        jnp.where((pc == 0) & first, turn_x(-1), px),
        jnp.where(pc == 0, turn_z(-1), pz),
        1 - pc,
    )
    far = tuple(jnp.where(pc == 1, a, b) for a, b in zip(right, left))
    partner = (g, px, pz, 1 - pc)
    direct = pz >= NZ - DIRECT

    def greet(x_at, z_at, c_at):
        pl.semaphore_signal(bar, inc=1, device_id=(g, x_at, z_at, c_at), device_id_type=MESH)

    greet(*far[1:])
    greet(px, pz, 1 - pc)
    for d in range(1, nx):
        for c in range(2):
            greet(turn_x(d), pz, c)

    @pl.when(pc == 1)
    def _():
        greet(px, turn_z(1), pc)
        greet(px, turn_z(-1), pc)

    @pl.when((pc == 1) & first)
    def _():
        for k in range(1, NZ):
            if k < NZ - DIRECT:
                greet(px, k, 1)
            else:
                for d in range(nx):
                    for c in range(2):
                        greet(turn_x(d), k, c)

    loads = [
        pltpu.make_async_copy(a, b, in_sem.at[i])
        for i, (a, b) in enumerate(((x_h, x), (tiles_h, tiles), (mass_h, mass), (src_h, src), (cols_h, cols)))
    ]
    for load in loads:
        load.start()
    from_roots = jnp.where(direct, nx, jnp.where((pc == 1) & jnp.logical_not(first), 1, 0))
    pl.semaphore_wait(bar, 2 * nx + jnp.where(pc == 1, 2, 0) + from_roots)

    def send(src, dst, ss, rs, to):
        copy = pltpu.make_async_remote_copy(src, dst, ss, rs, device_id=to, device_id_type=MESH)
        copy.start()
        return copy

    def landed(ref, sem):
        pltpu.make_async_copy(ref, ref, sem).wait()

    loads[0].wait()
    sent = [
        send(x.at[pl.ds(0, tile)], halo_x.at[1], x_ss.at[1], x_rs.at[1], left),
        send(x.at[pl.ds(tile, tile)], halo_x.at[0], x_ss.at[0], x_rs.at[0], right),
    ]
    for load in loads[1:]:
        load.wait()

    position = (px * NZ + pz) * 2 + pc
    parts = []
    for b in range(2):
        here = position * 2 + b
        found = []
        for d in (-1, 0, 1):
            found.append(sum((cols[b, k] == here + d).astype(F32) * tiles[b, k] for k in range(3)))
        parts.append(found)
    (t0l, t00, t01), (t10, t11, t1r) = parts
    eye = lax.broadcasted_iota(jnp.int32, (tile, tile), 0) == lax.broadcasted_iota(jnp.int32, (tile, tile), 1)
    ones = jnp.ones((tile, tile), BF16)
    diag = []
    for b in range(2):
        row = mass[pl.ds(b * tile, tile)].reshape(1, tile)
        rest = jnp.where(eye, row, 0.0) + (parts[b][0] + parts[b][1] + parts[b][2])
        high = rest.astype(BF16)
        rest = rest - high.astype(F32)
        mid = rest.astype(BF16)
        low = (rest - mid.astype(F32)).astype(BF16)
        diag.append(sum(jnp.dot(part, ones, preferred_element_type=F32) for part in (low, mid, high)))
    diag_first = diag[0]
    diag = jnp.concatenate(diag, axis=0)
    inner = halves(jnp.concatenate([jnp.concatenate([t00, t01], axis=1), jnp.concatenate([t10, t11], axis=1)], axis=0))
    to_left, to_right = halves(t0l), halves(t1r)

    x_pair = pair(x[...])
    ids = lax.broadcasted_iota(jnp.int32, (2 * tile, src.shape[0]), 0) + position * 2 * tile
    rhs = (ids == src[...].reshape(1, -1)).astype(F32)
    s = rhs - diag * x[...] + product(*inner, x_pair)
    s_buf[0] = s[:tile]
    s_buf[1] = s[tile:]
    m_buf[...] = jnp.where(eye, diag_first, 0.0) - t00
    from_left, from_right = halves(t0l.T), halves(t1r.T)
    sent += [
        send(s_buf.at[0], halo_s.at[1], s_ss.at[1], s_rs.at[1], left),
        send(s_buf.at[1], halo_s.at[0], s_ss.at[0], s_rs.at[0], right),
    ]
    to_chip = [
        pltpu.make_async_remote_copy(m_buf, halo_m, m_ss, m_rs, device_id=left, device_id_type=MESH),
        pltpu.make_async_remote_copy(q_buf, halo_q, q_ss, q_rs, device_id=left, device_id_type=MESH),
    ]

    @pl.when(pc == 0)
    def _():
        to_chip[0].start()
        landed(halo_x.at[1], x_rs.at[1])
        ahead = s[tile:] + product(*to_right, pair(halo_x[1]))
        whole = jnp.concatenate([s[:tile], ahead], axis=0)
        q_buf[...] = diag_first * s[:tile] - product(inner[0][:tile], inner[1][:tile], pair(whole))
        to_chip[1].start()

    on_left = product(*from_left, x_pair[:tile])
    on_right = product(*from_right, x_pair[tile:])

    @pl.when(pc == 1)
    def _():
        landed(halo_x.at[1], x_rs.at[1])

    landed(halo_x.at[0], x_rs.at[0])
    r = s + jnp.concatenate([product(*to_left, pair(halo_x[0])), product(*to_right, pair(halo_x[1]))], axis=0)
    r_pair = pair(r)
    near_r = diag * r - product(*inner, r_pair)
    back_r = [product(*from_left, r_pair[:tile]), product(*from_right, r_pair[tile:])]
    landed(halo_s.at[0], s_rs.at[0])
    landed(halo_s.at[1], s_rs.at[1])
    next_r = [halo_s[0] + on_left, halo_s[1] + on_right]
    w = near_r - jnp.concatenate([product(*to_left, pair(next_r[0])), product(*to_right, pair(next_r[1]))], axis=0)
    w_buf[0] = w[:tile]
    w_buf[1] = w[tile:]
    sent.append(send(w_buf.at[1 - pc], halo_w.at[pc], w_ss, w_rs, partner))

    w_pair = pair(w)
    sq, cross = rows_sum(r * r), rows_sum(r * w)
    ceiling = 2.0 * jnp.max(diag)
    about = jnp.where(sq > 0, jnp.clip(cross / sq, 0.0, ceiling), 0.0)
    u = w - about * r
    rss = rows_sum(u * u)
    near_u = diag * w - product(*inner, w_pair) - about * near_r
    back_u = [
        product(*from_left, w_pair[:tile]) - about * back_r[0],
        product(*from_right, w_pair[tile:]) - about * back_r[1],
    ]
    quad, lin, curv = rows_sum(u * near_u), 2.0 * rows_sum(r * near_u), rows_sum(r * near_r)

    @pl.when(pc == 0)
    def _():
        halo_w[0] = jnp.zeros_like(w_buf[0])

    @pl.when(pc == 1)
    def _():
        landed(halo_m, m_rs)
        across_m = product(*halves(halo_m[...]), pair(on_right)) - back_r[1]
        landed(halo_q, q_rs)
        halo_w[1] = halo_q[...] + across_m

    landed(halo_w.at[1 - pc], w_rs)
    for side, weight in ((0, pc.astype(F32)), (1, 1.0 + pc.astype(F32))):
        next_u = halo_w[side] - about * next_r[side]
        quad -= weight * rows_sum(back_u[side] * next_u)
        lin -= weight * rows_sum(back_u[side] * next_r[side] + back_r[side] * next_u)
        curv -= weight * rows_sum(back_r[side] * next_r[side])
    blank = jnp.zeros((1, sq.shape[1]), F32)
    mine = jnp.concatenate([sq, cross, about, rss, quad, lin, curv, blank], axis=0)
    own[...] = mine

    planes = NZ - DIRECT - 1
    slot = planes + jnp.where(direct, pz - planes, 0) * 2 * nx + px * 2 + pc
    to_plane = [
        pltpu.make_async_remote_copy(
            own, ranks.at[slot], p_ss.at[d], z_rs.at[slot],
            device_id=(g, turn_x(d), jnp.where(direct, 0, pz), 1), device_id_type=MESH,
        )
        for d in range(nx)
    ]
    for copy in to_plane[1:]:
        copy.start()

    @pl.when((pc == 0) | direct)
    def _():
        to_plane[0].start()

    rank = jnp.clip(pz - 1, 0, planes - 1)
    down = pltpu.make_async_remote_copy(
        plane_sum, ranks.at[rank], z_ss, z_rs.at[rank], device_id=(g, px, 0, 1), device_id_type=MESH
    )

    def pass_on(c, z_at, k):
        return pltpu.make_async_remote_copy(
            total, total, b_ss.at[k], b_rs, device_id=(g, px, z_at, c), device_id_type=MESH
        )

    half = NZ // 2
    across, up, back = pass_on(0, pz, 0), pass_on(1, turn_z(1), 1), pass_on(1, turn_z(-1), 2)

    @pl.when((pc == 1) & jnp.logical_not(direct))
    def _():
        ranks[slot] = mine
        for d in range(nx):
            for c in range(2):
                if (d, c) != (0, 1):
                    at = planes + turn_x(d) * 2 + c
                    landed(ranks.at[at], z_rs.at[at])

        @pl.when(jnp.logical_not(first))
        def _():
            plane_sum[...] = jnp.concatenate([*merged(ranks.at[pl.ds(planes, 2 * nx)]), blank], axis=0)
            down.start()

    @pl.when((pc == 1) & first)
    def _():
        for k in (*range(planes), *range(planes + 2 * nx, planes + 2 * nx * (DIRECT + 1))):
            landed(ranks.at[k], z_rs.at[k])
        sq, cross, _, rss, quad, _, _ = merged(ranks)
        step = sq / cross
        after = step * step * rss
        ratio = after / sq
        step_next = after / (step * step * quad - ratio * after / step)
        total[...] = jnp.concatenate(
            [step + step_next * (1.0 + ratio), -(step_next * step), jnp.zeros((6, sq.shape[1]), F32)], axis=0
        )

    @pl.when(jnp.logical_not((pc == 1) & first))
    def _():
        landed(total, b_rs)

    go_up, go_back = (pc == 1) & (pz < half), (pc == 1) & (first | (pz > half + 1))

    @pl.when(pc == 1)
    def _():
        across.start()

    @pl.when(go_up)
    def _():
        up.start()

    @pl.when(go_back)
    def _():
        back.start()

    out[...] = x[...] + total[0:1] * r + total[1:2] * w

    for copy in (*sent, *to_plane[1:]):
        copy.wait_send()

    for cond, copies in (
        (pc == 0, to_chip),
        ((pc == 0) | direct, to_plane[:1]),
        ((pc == 1) & jnp.logical_not(direct | first), [down]),
        (pc == 1, [across]),
        (go_up, [up]),
        (go_back, [back]),
    ):

        @pl.when(cond)
        def _(copies=copies):
            for copy in copies:
                copy.wait_send()


def body(block_cols, step_tiles, mass, warm_start, source_ids):
    nx = lax.axis_size("patch_0")
    tile = step_tiles.shape[-1]
    rows, width = warm_start.shape
    edge, square, sums = (2, tile, width), (tile, tile), (8, width)
    slots = NZ - DIRECT - 1 + 2 * nx * (DIRECT + 1)
    sem = pltpu.SemaphoreType.DMA
    return pl.pallas_call(
        functools.partial(kernel, nx, tile),
        out_shape=pltpu.VMEM((rows, width), F32),
        in_specs=[ANY] * 5,
        out_specs=pl.BlockSpec(memory_space=pltpu.VMEM),
        scratch_shapes=[
            pltpu.SMEM(block_cols.shape, jnp.int32),
            pltpu.VMEM(step_tiles.shape, F32),
            pltpu.VMEM(mass.shape, F32),
            pltpu.VMEM((rows, width), F32),
            pltpu.VMEM(source_ids.shape, jnp.int32),
            pltpu.VMEM(edge, F32), pltpu.VMEM(edge, F32), pltpu.VMEM(edge, F32),
            pltpu.VMEM(square, F32), pltpu.VMEM((tile, width), F32),
            pltpu.VMEM(edge, F32), pltpu.VMEM(edge, F32),
            pltpu.VMEM(square, F32), pltpu.VMEM((tile, width), F32),
            pltpu.VMEM(sums, F32),
            pltpu.VMEM((slots, *sums), F32),
            pltpu.VMEM(sums, F32),
            pltpu.VMEM(sums, F32),
            sem((5,)),
            sem((2,)), sem((2,)),
            sem((2,)), sem((2,)),
            sem, sem,
            sem, sem,
            sem, sem,
            sem((nx,)),
            sem, sem((slots,)),
            sem((3,)), sem,
        ],
        compiler_params=pltpu.CompilerParams(collective_id=0, has_side_effects=True),
        name="heat",
    )(block_cols, step_tiles, mass, warm_start, source_ids)


def solution(mesh):
    split = Mesh(
        mesh.devices.reshape(mesh.shape["groups"], mesh.shape["patch"] // NZ, NZ, mesh.shape["sub"]), AXES
    )
    placed = (P(AXES, None), P(AXES, None, None, None), P(AXES), P(AXES, None), P("groups"))
    return jax.shard_map(body, mesh=split, in_specs=placed, out_specs=P(AXES, None), check_vma=False)
```

time: 66.5 us -> 60.6 us (0.911)
  Pallas kernels: 62.8 us -> 58.7 us
  other arithmetic: 1.64 us -> 0 us
    pallas_call x1, Pallas kernels: 62.8 us -> 58.7 us  [body(): pl.pallas_call(functools.partial(kernel, nx, tile), out_shape=pltpu.VMEM(...]
    add x1 -> x0, other arithmetic: 1.64 us -> none  [body(): return warm_start + co[0:1] * r + co[1:2] * w]
    mul x1 -> x0, local copies, waits for them, and re-layouts: 0.76 us -> none  [body(): return warm_start + co[0:1] * r + co[1:2] * w]
where the time goes in v2:
time: 60.6 us; the launch traced here: 59.4 us
  Pallas kernels  58.7 us (97%)
  local copies, waits for them, and re-layouts  0.66 us (1%)
    pallas_call x1, Pallas kernels, body(): pl.pallas_call(functools.partial(kernel, nx, tile), out_shape=pltpu.VMEM(...  58.7 us

profile of v2, /device:TPU:40, one launch (start us, length us, event | category | flops | bytes accessed | tf_op | source)
XLA Modules:
  0.0 59.4 jit_solution(5048250641324105504)
XLA Ops:
  0.0 58.7 %heat.1 = f32[256,128]{1,0:T(8,128)S(1)} custom-call(s32[2,3]{1,0:T(2,128)} %cols_h.1, f32[2,3,128,128]{3,2,1,0:T(8,128)} %tiles_h.1, f32[256]{0:T(256)} %mass_h.1, f32[256,128]{1,0:T(8,128)} %x_h.1, s32[128]{0:T(128)} %src_h.1), custom_call_target="tpu_custom_call" | custom-call | tf_op jit(solution)/shard_map/heat/pallas_call | solution.py:339
  58.7 0.7 %copy.7 = f32[256,128]{1,0:T(8,128)} copy(f32[256,128]{1,0:T(8,128)S(1)} %heat.1) | data formatting | bytes 262144

commit v3 on v2

v3 whole, which is shorter than its diff:
```python
import functools

import jax
import jax.numpy as jnp
from jax import lax
from jax.experimental import pallas as pl
from jax.experimental.pallas import tpu as pltpu
from jax.sharding import Mesh
from jax.sharding import PartitionSpec as P

NZ = 32
AXES = ("groups", "patch_0", "patch_1", "sub")
MESH = pl.DeviceIdType.MESH
F32, BF16 = jnp.float32, jnp.bfloat16
ANY = pl.BlockSpec(memory_space=pl.ANY)


def halves(value):
    high = value.astype(BF16)
    return high, (value - high.astype(F32)).astype(BF16)


def pair(value):
    return jnp.concatenate(halves(value), axis=1)


def product(high, low, packed):
    n = packed.shape[1] // 2
    both = jnp.dot(high, packed, preferred_element_type=F32) + jnp.dot(low, packed, preferred_element_type=F32)
    return both[:, :n] + both[:, n:]


def rows_sum(value):
    return jnp.sum(value, axis=0, keepdims=True)


def merged(buf):
    sq, cross, about, rss, quad, lin, curv = (buf[:, k, :] for k in range(7))
    sq_all, cross_all = rows_sum(sq), rows_sum(cross)
    centre = jnp.where(sq_all > 0, cross_all / sq_all, 0.0)
    off = about - centre
    first = cross - about * sq
    rss_all = rows_sum(rss + off * (2.0 * first + off * sq))
    quad_all = rows_sum(quad + off * (lin + off * curv))
    lin_all = rows_sum(lin + 2.0 * off * curv)
    return sq_all, cross_all, centre, rss_all, quad_all, lin_all, rows_sum(curv)


def kernel(
    nx, tile,
    cols_h, tiles_h, mass_h, x_h, src_h,
    out,
    cols, tiles, mass, x, src,
    halo_x, halo_s, halo_w, halo_m, halo_q, s_buf, w_buf, m_buf, q_buf, own, ranks, line, lines, total,
    in_sem, x_ss, x_rs, s_ss, s_rs, w_ss, w_rs, m_ss, m_rs, q_ss, q_rs, z_ss, z_rs, l_ss, l_rs, b_ss, b_rs,
):
    g, px, pz, pc = (lax.axis_index(name) for name in AXES)
    bar = pltpu.get_barrier_semaphore()

    def turn_x(d):
        return lax.rem(px + d + nx, nx)

    def turn_z(d):
        return lax.rem(pz + d + NZ, NZ)

    first, last = pz == 0, pz == NZ - 1
    right = (
        g,
        jnp.where((pc == 1) & last, turn_x(1), px),
        jnp.where(pc == 1, turn_z(1), pz),
        1 - pc,
    )
    left = (
        g,
        jnp.where((pc == 0) & first, turn_x(-1), px),
        jnp.where(pc == 0, turn_z(-1), pz),
        1 - pc,
    )
    far = tuple(jnp.where(pc == 1, a, b) for a, b in zip(right, left))
    partner = (g, px, pz, 1 - pc)
    is_root = first & (pc == 1)

    loads = [
        pltpu.make_async_copy(a, b, in_sem.at[i])
        for i, (a, b) in enumerate(((x_h, x), (tiles_h, tiles), (mass_h, mass), (src_h, src), (cols_h, cols)))
    ]
    for load in loads:
        load.start()

    def greet(x_at, z_at, c_at):
        pl.semaphore_signal(bar, inc=1, device_id=(g, x_at, z_at, c_at), device_id_type=MESH)

    greet(*partner[1:])
    greet(*far[1:])

    @pl.when(is_root)
    def _():
        for d in range(1, nx):
            greet(turn_x(d), pz, 1)

        def greet_line(k, carry):
            greet(px, NZ - k, 0)
            greet(px, NZ - k, 1)
            return carry

        lax.fori_loop(1, NZ, greet_line, 0)

    pl.semaphore_wait(bar, 2 + jnp.where(is_root, nx - 1, jnp.where(first, 0, 1)))

    def send(src, dst, ss, rs, to):
        copy = pltpu.make_async_remote_copy(src, dst, ss, rs, device_id=to, device_id_type=MESH)
        copy.start()
        return copy

    def landed(ref, sem):
        pltpu.make_async_copy(ref, ref, sem).wait()

    loads[0].wait()
    sent = [
        send(x.at[pl.ds(0, tile)], halo_x.at[1], x_ss.at[1], x_rs.at[1], left),
        send(x.at[pl.ds(tile, tile)], halo_x.at[0], x_ss.at[0], x_rs.at[0], right),
    ]
    for load in loads[1:]:
        load.wait()

    position = (px * NZ + pz) * 2 + pc
    parts = []
    for b in range(2):
        here = position * 2 + b
        found = []
        for d in (-1, 0, 1):
            found.append(sum((cols[b, k] == here + d).astype(F32) * tiles[b, k] for k in range(3)))
        parts.append(found)
    (t0l, t00, t01), (t10, t11, t1r) = parts
    eye = lax.broadcasted_iota(jnp.int32, (tile, tile), 0) == lax.broadcasted_iota(jnp.int32, (tile, tile), 1)
    ones = jnp.ones((tile, tile), BF16)
    diag = []
    for b in range(2):
        row = mass[pl.ds(b * tile, tile)].reshape(1, tile)
        rest = jnp.where(eye, row, 0.0) + (parts[b][0] + parts[b][1] + parts[b][2])
        high = rest.astype(BF16)
        rest = rest - high.astype(F32)
        mid = rest.astype(BF16)
        low = (rest - mid.astype(F32)).astype(BF16)
        diag.append(sum(jnp.dot(part, ones, preferred_element_type=F32) for part in (low, mid, high)))
    diag_last = diag[1]
    diag = jnp.concatenate(diag, axis=0)
    inner = halves(jnp.concatenate([jnp.concatenate([t00, t01], axis=1), jnp.concatenate([t10, t11], axis=1)], axis=0))
    to_left, to_right = halves(t0l), halves(t1r)

    x_pair = pair(x[...])
    ids = lax.broadcasted_iota(jnp.int32, (2 * tile, src.shape[0]), 0) + position * 2 * tile
    rhs = (ids == src[...].reshape(1, -1)).astype(F32)
    s = rhs - diag * x[...] + product(*inner, x_pair)
    s_buf[0] = s[:tile]
    s_buf[1] = s[tile:]
    m_buf[...] = jnp.where(eye, diag_last, 0.0) - t11
    from_left, from_right = halves(t0l.T), halves(t1r.T)
    sent += [
        send(s_buf.at[0], halo_s.at[1], s_ss.at[1], s_rs.at[1], left),
        send(s_buf.at[1], halo_s.at[0], s_ss.at[0], s_rs.at[0], right),
    ]
    to_chip = [
        pltpu.make_async_remote_copy(m_buf, halo_m, m_ss, m_rs, device_id=right, device_id_type=MESH),
        pltpu.make_async_remote_copy(q_buf, halo_q, q_ss, q_rs, device_id=right, device_id_type=MESH),
    ]

    @pl.when(pc == 1)
    def _():
        to_chip[0].start()
        landed(halo_x.at[0], x_rs.at[0])
        behind = s[:tile] + product(*to_left, pair(halo_x[0]))
        whole = jnp.concatenate([behind, s[tile:]], axis=0)
        q_buf[...] = diag_last * s[tile:] - product(inner[0][tile:], inner[1][tile:], pair(whole))
        to_chip[1].start()

    on_left = product(*from_left, x_pair[:tile])
    on_right = product(*from_right, x_pair[tile:])

    @pl.when(pc == 0)
    def _():
        landed(halo_x.at[0], x_rs.at[0])

    landed(halo_x.at[1], x_rs.at[1])
    r = s + jnp.concatenate([product(*to_left, pair(halo_x[0])), product(*to_right, pair(halo_x[1]))], axis=0)
    r_pair = pair(r)
    near_r = diag * r - product(*inner, r_pair)
    back_r = product(*from_left, r_pair[:tile])
    landed(halo_s.at[0], s_rs.at[0])
    landed(halo_s.at[1], s_rs.at[1])
    next_r = [halo_s[0] + on_left, halo_s[1] + on_right]
    w = near_r - jnp.concatenate([product(*to_left, pair(next_r[0])), product(*to_right, pair(next_r[1]))], axis=0)
    to_core = pltpu.make_async_remote_copy(
        w_buf, halo_w, w_ss, w_rs, device_id=partner, device_id_type=MESH
    )

    @pl.when(pc == 0)
    def _():
        w_buf[...] = w[tile:]
        to_core.start()


    w_pair = pair(w)
    sq, cross = rows_sum(r * r), rows_sum(r * w)
    ceiling = 2.0 * jnp.max(diag)
    about = jnp.where(sq > 0, jnp.clip(cross / sq, 0.0, ceiling), 0.0)
    u = w - about * r
    rss = rows_sum(u * u)
    near_u = diag * w - product(*inner, w_pair) - about * near_r
    back_u = product(*from_left, w_pair[:tile]) - about * back_r
    quad, lin, curv = rows_sum(u * near_u), 2.0 * rows_sum(r * near_u), rows_sum(r * near_r)

    @pl.when(pc == 0)
    def _():
        landed(halo_m, m_rs)
        across_m = product(*halves(halo_m[...]), pair(on_left)) - back_r
        landed(halo_q, q_rs)
        halo_w[...] = halo_q[...] + across_m

    @pl.when(pc == 1)
    def _():
        landed(halo_w, w_rs)

    next_u = halo_w[...] - about * next_r[0]
    quad -= 2.0 * rows_sum(back_u * next_u)
    lin -= 2.0 * rows_sum(back_u * next_r[0] + back_r * next_u)
    curv -= 2.0 * rows_sum(back_r * next_r[0])
    blank = jnp.zeros((1, sq.shape[1]), F32)
    mine = jnp.concatenate([sq, cross, about, rss, quad, lin, curv, blank], axis=0)
    own[...] = mine

    slot = pz * 2 + pc
    to_root = pltpu.make_async_remote_copy(
        own, ranks.at[slot], z_ss, z_rs.at[slot], device_id=(g, px, 0, 1), device_id_type=MESH
    )
    to_lines = [
        pltpu.make_async_remote_copy(
            line, lines.at[px], l_ss.at[d], l_rs.at[px], device_id=(g, turn_x(d), pz, 1), device_id_type=MESH
        )
        for d in range(1, nx)
    ]
    to_partner = pltpu.make_async_remote_copy(
        total, total, b_ss.at[0], b_rs, device_id=partner, device_id_type=MESH
    )

    def to_all(k, act):
        for c in range(2):
            act(
                pltpu.make_async_remote_copy(
                    total, total, b_ss.at[2 * k + c], b_rs, device_id=(g, px, k, c), device_id_type=MESH
                )
            )

    def along(act):
        def step(k, carry):
            to_all(k, act)
            to_all(NZ - k, act)
            return carry

        lax.fori_loop(1, NZ // 2, step, 0)
        to_all(NZ // 2, act)

    @pl.when(is_root)
    def _():
        ranks[1] = mine
        for k in range(2 * NZ):
            if k != 1:
                landed(ranks.at[k], z_rs.at[k])
        joined = jnp.concatenate([*merged(ranks), blank], axis=0)
        line[...] = joined
        lines[px] = joined
        for copy in to_lines:
            copy.start()
        for d in range(1, nx):
            landed(lines.at[turn_x(d)], l_rs.at[turn_x(d)])
        sq, cross, _, rss, quad, _, _ = merged(lines)
        step = sq / cross
        after = step * step * rss
        ratio = after / sq
        step_next = after / (step * step * quad - ratio * after / step)
        total[...] = jnp.concatenate([step + step_next * (1.0 + ratio), -(step_next * step)], axis=0)
        to_partner.start()

    @pl.when(jnp.logical_not(is_root))
    def _():
        to_root.start()
        landed(total, b_rs)

    is_caster = first & (pc == 0)

    @pl.when(is_caster)
    def _():
        along(lambda copy: copy.start())

    out[...] = x[...] + total[0:1] * r + total[1:2] * w

    for copy in sent:
        copy.wait_send()

    @pl.when(pc == 0)
    def _():
        to_core.wait_send()

    @pl.when(pc == 1)
    def _():
        for copy in to_chip:
            copy.wait_send()

    @pl.when(is_root)
    def _():
        for copy in (*to_lines, to_partner):
            copy.wait_send()

    @pl.when(jnp.logical_not(is_root))
    def _():
        to_root.wait_send()

    @pl.when(is_caster)
    def _():
        along(lambda copy: copy.wait_send())


def body(block_cols, step_tiles, mass, warm_start, source_ids):
    nx = lax.axis_size("patch_0")
    tile = step_tiles.shape[-1]
    rows, width = warm_start.shape
    edge, square, sums = (2, tile, width), (tile, tile), (8, width)
    sem = pltpu.SemaphoreType.DMA
    return pl.pallas_call(
        functools.partial(kernel, nx, tile),
        out_shape=pltpu.VMEM((rows, width), F32),
        in_specs=[ANY] * 5,
        out_specs=pl.BlockSpec(memory_space=pltpu.VMEM),
        scratch_shapes=[
            pltpu.SMEM(block_cols.shape, jnp.int32),
            pltpu.VMEM(step_tiles.shape, F32),
            pltpu.VMEM(mass.shape, F32),
            pltpu.VMEM((rows, width), F32),
            pltpu.VMEM(source_ids.shape, jnp.int32),
            pltpu.VMEM(edge, F32), pltpu.VMEM(edge, F32), pltpu.VMEM(edge[1:], F32),
            pltpu.VMEM(square, F32), pltpu.VMEM(edge[1:], F32),
            pltpu.VMEM(edge, F32), pltpu.VMEM(edge[1:], F32),
            pltpu.VMEM(square, F32), pltpu.VMEM(edge[1:], F32),
            pltpu.VMEM(sums, F32),
            pltpu.VMEM((2 * NZ, *sums), F32),
            pltpu.VMEM(sums, F32),
            pltpu.VMEM((nx, *sums), F32),
            pltpu.VMEM((2, width), F32),
            sem((5,)),
            sem((2,)), sem((2,)),
            sem((2,)), sem((2,)),
            sem, sem,
            sem, sem,
            sem, sem,
            sem, sem((2 * NZ,)),
            sem((nx,)), sem((nx,)),
            sem((2 * NZ,)), sem,
        ],
        compiler_params=pltpu.CompilerParams(collective_id=0, has_side_effects=True),
        name="heat",
    )(block_cols, step_tiles, mass, warm_start, source_ids)


def solution(mesh):
    split = Mesh(
        mesh.devices.reshape(mesh.shape["groups"], mesh.shape["patch"] // NZ, NZ, mesh.shape["sub"]), AXES
    )
    placed = (P(AXES, None), P(AXES, None, None, None), P(AXES), P(AXES, None), P("groups"))
    return jax.shard_map(body, mesh=split, in_specs=placed, out_specs=P(AXES, None), check_vma=False)
```

time: 60.6 us -> 62.2 us (1.026); the launches traced: 59.4 us -> 62.1 us
  Pallas kernels: 58.7 us -> 61.5 us
    pallas_call x1, Pallas kernels: 58.7 us -> 61.5 us  [body(): pl.pallas_call(functools.partial(kernel, nx, tile), out_shape=pltpu.VMEM(...]
where the time goes in v3:
time: 62.2 us; the launch traced here: 62.1 us
  Pallas kernels  61.5 us (99%)
  local copies, waits for them, and re-layouts  0.66 us (1%)
    pallas_call x1, Pallas kernels, body(): pl.pallas_call(functools.partial(kernel, nx, tile), out_shape=pltpu.VMEM(...  61.5 us

profile of v3, /device:TPU:40, one launch (start us, length us, event | category | flops | bytes accessed | tf_op | source)
XLA Modules:
  0.0 62.1 jit_solution(6502572408400034431)
XLA Ops:
  0.0 61.5 %heat.1 = f32[256,128]{1,0:T(8,128)S(1)} custom-call(s32[2,3]{1,0:T(2,128)} %cols_h.1, f32[2,3,128,128]{3,2,1,0:T(8,128)} %tiles_h.1, f32[256]{0:T(256)} %mass_h.1, f32[256,128]{1,0:T(8,128)} %x_h.1, s32[128]{0:T(128)} %src_h.1), custom_call_target="tpu_custom_call" | custom-call | tf_op jit(solution)/shard_map/heat/pallas_call | solution.py:329
  61.5 0.7 %copy.7 = f32[256,128]{1,0:T(8,128)} copy(f32[256,128]{1,0:T(8,128)S(1)} %heat.1) | data formatting | bytes 262144

commit v4 on v3

--- a/solution.py
+++ b/solution.py
@@ -51,8 +51,9 @@
     cols_h, tiles_h, mass_h, x_h, src_h,
     out,
     cols, tiles, mass, x, src,
-    halo_x, halo_s, halo_w, halo_m, halo_q, s_buf, w_buf, m_buf, q_buf, own, ranks, line, lines, total,
-    in_sem, x_ss, x_rs, s_ss, s_rs, w_ss, w_rs, m_ss, m_rs, q_ss, q_rs, z_ss, z_rs, l_ss, l_rs, b_ss, b_rs,
+    halo_x, halo_s, halo_w, halo_m, halo_q, s_buf, w_buf, m_buf, q_buf, own, ranks, line, late, total,
+    in_sem, x_ss, x_rs, s_ss, s_rs, w_ss, w_rs, m_ss, m_rs, q_ss, q_rs, pass_ss, up_sem,
+    z_ss, z_rs, l_ss, l_rs, b_ss, b_rs,
 ):
     g, px, pz, pc = (lax.axis_index(name) for name in AXES)
     bar = pltpu.get_barrier_semaphore()
@@ -64,21 +65,13 @@
         return lax.rem(pz + d + NZ, NZ)
 
     first, last = pz == 0, pz == NZ - 1
-    right = (
-        g,
-        jnp.where((pc == 1) & last, turn_x(1), px),
-        jnp.where(pc == 1, turn_z(1), pz),
-        1 - pc,
-    )
-    left = (
-        g,
-        jnp.where((pc == 0) & first, turn_x(-1), px),
-        jnp.where(pc == 0, turn_z(-1), pz),
-        1 - pc,
-    )
+    right = (g, jnp.where((pc == 1) & last, turn_x(1), px), jnp.where(pc == 1, turn_z(1), pz), 1 - pc)
+    left = (g, jnp.where((pc == 0) & first, turn_x(-1), px), jnp.where(pc == 0, turn_z(-1), pz), 1 - pc)
     far = tuple(jnp.where(pc == 1, a, b) for a, b in zip(right, left))
     partner = (g, px, pz, 1 - pc)
-    is_root = first & (pc == 1)
+    is_root, is_caster, is_end = first & (pc == 1), first & (pc == 0), last & (pc == 1)
+    by_way = (g, jnp.where(is_caster, turn_x(-1), left[1]), jnp.where(is_caster, 0, left[2]), left[3])
+    way_slot = jnp.where(is_caster, 2, 1)
 
     loads = [
         pltpu.make_async_copy(a, b, in_sem.at[i])
@@ -91,21 +84,32 @@
         pl.semaphore_signal(bar, inc=1, device_id=(g, x_at, z_at, c_at), device_id_type=MESH)
 
     greet(*partner[1:])
-    greet(*far[1:])
+
+    @pl.when(jnp.logical_not(is_end))
+    def _():
+        greet(*far[1:])
+
+    @pl.when(first)
+    def _():
+        for d in range(nx):
+            for c in range(2):
+                greet(turn_x(d), NZ - 1, c)
+                if d > 0:
+                    greet(turn_x(d), 0, c)
 
     @pl.when(is_root)
     def _():
-        for d in range(1, nx):
-            greet(turn_x(d), pz, 1)
-
         def greet_line(k, carry):
-            greet(px, NZ - k, 0)
-            greet(px, NZ - k, 1)
+            greet(px, NZ - 1 - k, 0)
+            greet(px, NZ - 1 - k, 1)
             return carry
 
-        lax.fori_loop(1, NZ, greet_line, 0)
-
-    pl.semaphore_wait(bar, 2 + jnp.where(is_root, nx - 1, jnp.where(first, 0, 1)))
+        lax.fori_loop(1, NZ - 1, greet_line, 0)
+
+    mates = 2 * nx - 1
+    pl.semaphore_wait(
+        bar, jnp.where(first, mates + jnp.where(is_root, 1, 0), jnp.where(last, 2 + 2 * nx, 3))
+    )
 
     def send(src, dst, ss, rs, to):
         copy = pltpu.make_async_remote_copy(src, dst, ss, rs, device_id=to, device_id_type=MESH)
@@ -115,9 +119,13 @@
     def landed(ref, sem):
         pltpu.make_async_copy(ref, ref, sem).wait()
 
+    @pl.when(is_end)
+    def _():
+        pl.semaphore_signal(up_sem, inc=1, device_id=(g, px, 0, 1), device_id_type=MESH)
+
     loads[0].wait()
     sent = [
-        send(x.at[pl.ds(0, tile)], halo_x.at[1], x_ss.at[1], x_rs.at[1], left),
+        send(x.at[pl.ds(0, tile)], halo_x.at[way_slot], x_ss.at[1], x_rs.at[way_slot], by_way),
         send(x.at[pl.ds(tile, tile)], halo_x.at[0], x_ss.at[0], x_rs.at[0], right),
     ]
     for load in loads[1:]:
@@ -157,13 +165,28 @@
     m_buf[...] = jnp.where(eye, diag_last, 0.0) - t11
     from_left, from_right = halves(t0l.T), halves(t1r.T)
     sent += [
-        send(s_buf.at[0], halo_s.at[1], s_ss.at[1], s_rs.at[1], left),
+        send(s_buf.at[0], halo_s.at[way_slot], s_ss.at[1], s_rs.at[way_slot], by_way),
         send(s_buf.at[1], halo_s.at[0], s_ss.at[0], s_rs.at[0], right),
     ]
     to_chip = [
         pltpu.make_async_remote_copy(m_buf, halo_m, m_ss, m_rs, device_id=right, device_id_type=MESH),
         pltpu.make_async_remote_copy(q_buf, halo_q, q_ss, q_rs, device_id=right, device_id_type=MESH),
     ]
+
+    passed = [
+        pltpu.make_async_remote_copy(
+            ref.at[2], ref.at[1], pass_ss.at[i], rs.at[1], device_id=(g, px, NZ - 1, 1), device_id_type=MESH
+        )
+        for i, (ref, rs) in enumerate(((halo_x, x_rs), (halo_s, s_rs)))
+    ]
+
+    @pl.when(is_root)
+    def _():
+        landed(halo_x.at[2], x_rs.at[2])
+        landed(halo_s.at[2], s_rs.at[2])
+        pl.semaphore_wait(up_sem, 1)
+        for copy in passed:
+            copy.start()
 
     @pl.when(pc == 1)
     def _():
@@ -229,68 +252,88 @@
     mine = jnp.concatenate([sq, cross, about, rss, quad, lin, curv, blank], axis=0)
     own[...] = mine
 
-    slot = pz * 2 + pc
-    to_root = pltpu.make_async_remote_copy(
-        own, ranks.at[slot], z_ss, z_rs.at[slot], device_id=(g, px, 0, 1), device_id_type=MESH
+    edge_plane = first | last
+    slot = jnp.where(edge_plane, nx + jnp.where(first, 2 * nx, 0) + px * 2 + pc, 0)
+    rank = jnp.where(edge_plane, 0, (pz - 1) * 2 + pc)
+    others = [(d, c) for d in (2, 1, nx - 1, 0) for c in range(2) if (d, c) != (0, 0)]
+
+    def share(src, at, ss, targets):
+        return [
+            pltpu.make_async_remote_copy(
+                src, late.at[at], ss, l_rs, device_id=(g, turn_x(d), 0, lax.rem(pc + c, 2)), device_id_type=MESH
+            )
+            for d, c in targets
+        ]
+
+    mine_out, line_out = share(own, slot, z_ss, others), share(line, px, l_ss, others)
+    (mine_down,) = share(own, slot, z_ss, [(0, 0)])
+    mine_to_root = pltpu.make_async_remote_copy(
+        own, ranks.at[rank], z_ss, z_rs, device_id=(g, px, 0, 1), device_id_type=MESH
     )
-    to_lines = [
-        pltpu.make_async_remote_copy(
-            line, lines.at[px], l_ss.at[d], l_rs.at[px], device_id=(g, turn_x(d), pz, 1), device_id_type=MESH
-        )
-        for d in range(1, nx)
-    ]
-    to_partner = pltpu.make_async_remote_copy(
-        total, total, b_ss.at[0], b_rs, device_id=partner, device_id_type=MESH
-    )
-
-    def to_all(k, act):
-        for c in range(2):
-            act(
-                pltpu.make_async_remote_copy(
-                    total, total, b_ss.at[2 * k + c], b_rs, device_id=(g, px, k, c), device_id_type=MESH
-                )
-            )
-
-    def along(act):
-        def step(k, carry):
-            to_all(k, act)
-            to_all(NZ - k, act)
-            return carry
-
-        lax.fori_loop(1, NZ // 2, step, 0)
-        to_all(NZ // 2, act)
+
+    @pl.when(edge_plane)
+    def _():
+        for copy in mine_out:
+            copy.start()
+
+    @pl.when(last)
+    def _():
+        mine_down.start()
+
+    @pl.when(jnp.logical_not(edge_plane))
+    def _():
+        mine_to_root.start()
+
+    count = 5 * nx
 
     @pl.when(is_root)
     def _():
-        ranks[1] = mine
-        for k in range(2 * NZ):
-            if k != 1:
-                landed(ranks.at[k], z_rs.at[k])
-        joined = jnp.concatenate([*merged(ranks), blank], axis=0)
+        inner_planes = ranks.at[pl.ds(0, 2 * NZ - 4)]
+        landed(inner_planes, z_rs)
+        joined = jnp.concatenate([*merged(inner_planes), blank], axis=0)
         line[...] = joined
-        lines[px] = joined
-        for copy in to_lines:
+        for copy in line_out:
             copy.start()
-        for d in range(1, nx):
-            landed(lines.at[turn_x(d)], l_rs.at[turn_x(d)])
-        sq, cross, _, rss, quad, _, _ = merged(lines)
+        late[px] = joined
+        late[slot] = mine
+        landed(late.at[pl.ds(0, count - 2)], l_rs)
+
+    @pl.when(is_caster)
+    def _():
+        late[slot] = mine
+        landed(late.at[pl.ds(0, count - 1)], l_rs)
+
+    def to_line(k):
+        return [
+            pltpu.make_async_remote_copy(total, total, b_ss, b_rs, device_id=(g, px, k, c), device_id_type=MESH)
+            for c in (1, 0)
+        ]
+
+    @pl.when(first)
+    def _():
+        sq, cross, _, rss, quad, _, _ = merged(late)
         step = sq / cross
         after = step * step * rss
         ratio = after / sq
         step_next = after / (step * step * quad - ratio * after / step)
-        total[...] = jnp.concatenate([step + step_next * (1.0 + ratio), -(step_next * step)], axis=0)
-        to_partner.start()
-
-    @pl.when(jnp.logical_not(is_root))
-    def _():
-        to_root.start()
+        total[...] = jnp.concatenate(
+            [step + step_next * (1.0 + ratio), -(step_next * step), jnp.zeros((6, sq.shape[1]), F32)], axis=0
+        )
+
+    @pl.when(jnp.logical_not(first))
+    def _():
         landed(total, b_rs)
 
-    is_caster = first & (pc == 0)
-
     @pl.when(is_caster)
     def _():
-        along(lambda copy: copy.start())
+        def step(k, carry):
+            for copy in (*to_line(k), *to_line(NZ - k)):
+                copy.start()
+            return carry
+
+        lax.fori_loop(1, NZ // 2, step, 0)
+        for copy in to_line(NZ // 2):
+            copy.start()
 
     out[...] = x[...] + total[0:1] * r + total[1:2] * w
 
@@ -306,25 +349,34 @@
         for copy in to_chip:
             copy.wait_send()
 
+    @pl.when(first)
+    def _():
+        landed(late.at[pl.ds(0, mates)], z_ss)
+
+    @pl.when(last)
+    def _():
+        landed(late.at[pl.ds(0, mates + 1)], z_ss)
+
+    @pl.when(jnp.logical_not(edge_plane))
+    def _():
+        mine_to_root.wait_send()
+
     @pl.when(is_root)
     def _():
-        for copy in (*to_lines, to_partner):
+        landed(late.at[pl.ds(0, mates)], l_ss)
+        for copy in passed:
             copy.wait_send()
 
-    @pl.when(jnp.logical_not(is_root))
-    def _():
-        to_root.wait_send()
-
     @pl.when(is_caster)
     def _():
-        along(lambda copy: copy.wait_send())
+        landed(ranks, b_ss)
 
 
 def body(block_cols, step_tiles, mass, warm_start, source_ids):
     nx = lax.axis_size("patch_0")
     tile = step_tiles.shape[-1]
     rows, width = warm_start.shape
-    edge, square, sums = (2, tile, width), (tile, tile), (8, width)
+    edge, slots, square, sums = (2, tile, width), (3, tile, width), (tile, tile), (8, width)
     sem = pltpu.SemaphoreType.DMA
     return pl.pallas_call(
         functools.partial(kernel, nx, tile),
@@ -337,24 +389,25 @@
             pltpu.VMEM(mass.shape, F32),
             pltpu.VMEM((rows, width), F32),
             pltpu.VMEM(source_ids.shape, jnp.int32),
-            pltpu.VMEM(edge, F32), pltpu.VMEM(edge, F32), pltpu.VMEM(edge[1:], F32),
+            pltpu.VMEM(slots, F32), pltpu.VMEM(slots, F32), pltpu.VMEM(edge[1:], F32),
             pltpu.VMEM(square, F32), pltpu.VMEM(edge[1:], F32),
             pltpu.VMEM(edge, F32), pltpu.VMEM(edge[1:], F32),
             pltpu.VMEM(square, F32), pltpu.VMEM(edge[1:], F32),
             pltpu.VMEM(sums, F32),
-            pltpu.VMEM((2 * NZ, *sums), F32),
+            pltpu.VMEM((2 * NZ - 2, *sums), F32),
             pltpu.VMEM(sums, F32),
-            pltpu.VMEM((nx, *sums), F32),
-            pltpu.VMEM((2, width), F32),
+            pltpu.VMEM((5 * nx, *sums), F32),
+            pltpu.VMEM(sums, F32),
             sem((5,)),
-            sem((2,)), sem((2,)),
-            sem((2,)), sem((2,)),
-            sem, sem,
-            sem, sem,
-            sem, sem,
-            sem, sem((2 * NZ,)),
-            sem((nx,)), sem((nx,)),
-            sem((2 * NZ,)), sem,
+            sem((2,)), sem((3,)),
+            sem((2,)), sem((3,)),
+            sem, sem,
+            sem, sem,
+            sem, sem,
+            sem((2,)), pltpu.SemaphoreType.REGULAR,
+            sem, sem,
+            sem, sem,
+            sem, sem,
         ],
         compiler_params=pltpu.CompilerParams(collective_id=0, has_side_effects=True),
         name="heat",

time: 62.2 us -> 59.6 us (0.958)
  Pallas kernels: 61.5 us -> 58.8 us
    pallas_call x1, Pallas kernels: 61.5 us -> 58.8 us  [body(): pl.pallas_call(functools.partial(kernel, nx, tile), out_shape=pltpu.VMEM(...]
where the time goes in v4:
time: 59.6 us; the launch traced here: 59.5 us
  Pallas kernels  58.8 us (99%)
  local copies, waits for them, and re-layouts  0.66 us (1%)
    pallas_call x1, Pallas kernels, body(): pl.pallas_call(functools.partial(kernel, nx, tile), out_shape=pltpu.VMEM(...  58.8 us

profile of v4, /device:TPU:40, one launch (start us, length us, event | category | flops | bytes accessed | tf_op | source)
XLA Modules:
  0.0 59.5 jit_solution(6224267333001948082)
XLA Ops:
  0.0 58.8 %heat.1 = f32[256,128]{1,0:T(8,128)S(1)} custom-call(s32[2,3]{1,0:T(2,128)} %cols_h.1, f32[2,3,128,128]{3,2,1,0:T(8,128)} %tiles_h.1, f32[256]{0:T(256)} %mass_h.1, f32[256,128]{1,0:T(8,128)} %x_h.1, s32[128]{0:T(128)} %src_h.1), custom_call_target="tpu_custom_call" | custom-call | tf_op jit(solution)/shard_map/heat/pallas_call | solution.py:381
  58.9 0.7 %copy.7 = f32[256,128]{1,0:T(8,128)} copy(f32[256,128]{1,0:T(8,128)S(1)} %heat.1) | data formatting | bytes 262144

commit v5 on v4

--- a/solution.py
+++ b/solution.py
@@ -9,6 +9,7 @@
 from jax.sharding import PartitionSpec as P
 
 NZ = 32
+NEAR = 4
 AXES = ("groups", "patch_0", "patch_1", "sub")
 MESH = pl.DeviceIdType.MESH
 F32, BF16 = jnp.float32, jnp.bfloat16
@@ -52,9 +53,9 @@
     out,
     cols, tiles, mass, x, src,
     halo_x, halo_s, halo_w, halo_m, halo_q, s_buf, w_buf, m_buf, q_buf, own, ranks, line, late, total,
-    in_sem, x_ss, x_rs, s_ss, s_rs, w_ss, w_rs, m_ss, m_rs, q_ss, q_rs, pass_ss, up_sem,
-    z_ss, z_rs, l_ss, l_rs, b_ss, b_rs,
+    in_sem, x_rs, s_rs, mw_rs, qz_rs, up_sem, l_rs,
 ):
+    large, small, passing = in_sem.at[0], in_sem.at[1], in_sem.at[2]
     g, px, pz, pc = (lax.axis_index(name) for name in AXES)
     bar = pltpu.get_barrier_semaphore()
 
@@ -112,9 +113,7 @@
     )
 
     def send(src, dst, ss, rs, to):
-        copy = pltpu.make_async_remote_copy(src, dst, ss, rs, device_id=to, device_id_type=MESH)
-        copy.start()
-        return copy
+        pltpu.make_async_remote_copy(src, dst, ss, rs, device_id=to, device_id_type=MESH).start()
 
     def landed(ref, sem):
         pltpu.make_async_copy(ref, ref, sem).wait()
@@ -124,10 +123,8 @@
         pl.semaphore_signal(up_sem, inc=1, device_id=(g, px, 0, 1), device_id_type=MESH)
 
     loads[0].wait()
-    sent = [
-        send(x.at[pl.ds(0, tile)], halo_x.at[way_slot], x_ss.at[1], x_rs.at[way_slot], by_way),
-        send(x.at[pl.ds(tile, tile)], halo_x.at[0], x_ss.at[0], x_rs.at[0], right),
-    ]
+    send(x.at[pl.ds(0, tile)], halo_x.at[way_slot], large, x_rs.at[way_slot], by_way)
+    send(x.at[pl.ds(tile, tile)], halo_x.at[0], large, x_rs.at[0], right)
     for load in loads[1:]:
         load.wait()
 
@@ -137,7 +134,7 @@
         here = position * 2 + b
         found = []
         for d in (-1, 0, 1):
-            found.append(sum((cols[b, k] == here + d).astype(F32) * tiles[b, k] for k in range(3)))
+            found.append(sum((cols[b, k] == here + d).astype(F32) * tiles[3 * b + k] for k in range(3)))
         parts.append(found)
     (t0l, t00, t01), (t10, t11, t1r) = parts
     eye = lax.broadcasted_iota(jnp.int32, (tile, tile), 0) == lax.broadcasted_iota(jnp.int32, (tile, tile), 1)
@@ -164,20 +161,18 @@
     s_buf[1] = s[tile:]
     m_buf[...] = jnp.where(eye, diag_last, 0.0) - t11
     from_left, from_right = halves(t0l.T), halves(t1r.T)
-    sent += [
-        send(s_buf.at[0], halo_s.at[way_slot], s_ss.at[1], s_rs.at[way_slot], by_way),
-        send(s_buf.at[1], halo_s.at[0], s_ss.at[0], s_rs.at[0], right),
-    ]
+    send(s_buf.at[0], halo_s.at[way_slot], large, s_rs.at[way_slot], by_way)
+    send(s_buf.at[1], halo_s.at[0], large, s_rs.at[0], right)
     to_chip = [
-        pltpu.make_async_remote_copy(m_buf, halo_m, m_ss, m_rs, device_id=right, device_id_type=MESH),
-        pltpu.make_async_remote_copy(q_buf, halo_q, q_ss, q_rs, device_id=right, device_id_type=MESH),
+        pltpu.make_async_remote_copy(m_buf, halo_m, large, mw_rs, device_id=right, device_id_type=MESH),
+        pltpu.make_async_remote_copy(q_buf, halo_q, large, qz_rs, device_id=right, device_id_type=MESH),
     ]
 
     passed = [
         pltpu.make_async_remote_copy(
-            ref.at[2], ref.at[1], pass_ss.at[i], rs.at[1], device_id=(g, px, NZ - 1, 1), device_id_type=MESH
+            ref.at[2], ref.at[1], passing, rs.at[1], device_id=(g, px, NZ - 1, 1), device_id_type=MESH
         )
-        for i, (ref, rs) in enumerate(((halo_x, x_rs), (halo_s, s_rs)))
+        for ref, rs in ((halo_x, x_rs), (halo_s, s_rs))
     ]
 
     @pl.when(is_root)
@@ -214,7 +209,7 @@
     next_r = [halo_s[0] + on_left, halo_s[1] + on_right]
     w = near_r - jnp.concatenate([product(*to_left, pair(next_r[0])), product(*to_right, pair(next_r[1]))], axis=0)
     to_core = pltpu.make_async_remote_copy(
-        w_buf, halo_w, w_ss, w_rs, device_id=partner, device_id_type=MESH
+        w_buf, halo_w, large, mw_rs, device_id=partner, device_id_type=MESH
     )
 
     @pl.when(pc == 0)
@@ -235,14 +230,14 @@
 
     @pl.when(pc == 0)
     def _():
-        landed(halo_m, m_rs)
+        landed(halo_m, mw_rs)
         across_m = product(*halves(halo_m[...]), pair(on_left)) - back_r
-        landed(halo_q, q_rs)
+        landed(halo_q, qz_rs)
         halo_w[...] = halo_q[...] + across_m
 
     @pl.when(pc == 1)
     def _():
-        landed(halo_w, w_rs)
+        landed(halo_w, mw_rs)
 
     next_u = halo_w[...] - about * next_r[0]
     quad -= 2.0 * rows_sum(back_u * next_u)
@@ -257,18 +252,18 @@
     rank = jnp.where(edge_plane, 0, (pz - 1) * 2 + pc)
     others = [(d, c) for d in (2, 1, nx - 1, 0) for c in range(2) if (d, c) != (0, 0)]
 
-    def share(src, at, ss, targets):
+    def share(src, at, targets):
         return [
             pltpu.make_async_remote_copy(
-                src, late.at[at], ss, l_rs, device_id=(g, turn_x(d), 0, lax.rem(pc + c, 2)), device_id_type=MESH
+                src, late.at[at], small, l_rs, device_id=(g, turn_x(d), 0, lax.rem(pc + c, 2)), device_id_type=MESH
             )
             for d, c in targets
         ]
 
-    mine_out, line_out = share(own, slot, z_ss, others), share(line, px, l_ss, others)
-    (mine_down,) = share(own, slot, z_ss, [(0, 0)])
+    mine_out, line_out = share(own, slot, others), share(line, px, others)
+    (mine_down,) = share(own, slot, [(0, 0)])
     mine_to_root = pltpu.make_async_remote_copy(
-        own, ranks.at[rank], z_ss, z_rs, device_id=(g, px, 0, 1), device_id_type=MESH
+        own, ranks.at[rank], small, qz_rs, device_id=(g, px, 0, 1), device_id_type=MESH
     )
 
     @pl.when(edge_plane)
@@ -289,7 +284,7 @@
     @pl.when(is_root)
     def _():
         inner_planes = ranks.at[pl.ds(0, 2 * NZ - 4)]
-        landed(inner_planes, z_rs)
+        landed(inner_planes, qz_rs)
         joined = jnp.concatenate([*merged(inner_planes), blank], axis=0)
         line[...] = joined
         for copy in line_out:
@@ -303,9 +298,9 @@
         late[slot] = mine
         landed(late.at[pl.ds(0, count - 1)], l_rs)
 
-    def to_line(k):
+    def to_chip_at(k):
         return [
-            pltpu.make_async_remote_copy(total, total, b_ss, b_rs, device_id=(g, px, k, c), device_id_type=MESH)
+            pltpu.make_async_remote_copy(total, total, small, l_rs, device_id=(g, px, k, c), device_id_type=MESH)
             for c in (1, 0)
         ]
 
@@ -322,54 +317,55 @@
 
     @pl.when(jnp.logical_not(first))
     def _():
-        landed(total, b_rs)
+        landed(total, l_rs)
+
+    is_second = last & (pc == 0)
 
     @pl.when(is_caster)
     def _():
+        for k in (*range(1, NEAR + 1), NZ - 1):
+            for copy in to_chip_at(k):
+                copy.start()
+
+    @pl.when(is_second)
+    def _():
         def step(k, carry):
-            for copy in (*to_line(k), *to_line(NZ - k)):
+            for copy in to_chip_at(k):
                 copy.start()
             return carry
 
-        lax.fori_loop(1, NZ // 2, step, 0)
-        for copy in to_line(NZ // 2):
-            copy.start()
+        lax.fori_loop(NEAR + 1, NZ - 1, step, 0)
 
     out[...] = x[...] + total[0:1] * r + total[1:2] * w
 
-    for copy in sent:
-        copy.wait_send()
-
     @pl.when(pc == 0)
     def _():
-        to_core.wait_send()
+        landed(tiles.at[pl.ds(0, 5)], large)
 
     @pl.when(pc == 1)
     def _():
-        for copy in to_chip:
-            copy.wait_send()
-
-    @pl.when(first)
-    def _():
-        landed(late.at[pl.ds(0, mates)], z_ss)
-
-    @pl.when(last)
-    def _():
-        landed(late.at[pl.ds(0, mates + 1)], z_ss)
+        landed(tiles, large)
+
+    @pl.when(is_root)
+    def _():
+        landed(halo_x.at[pl.ds(0, 2)], passing)
+        landed(ranks.at[pl.ds(0, 2 * mates)], small)
+
+    @pl.when(is_caster)
+    def _():
+        landed(ranks.at[pl.ds(0, mates + 2 * (NEAR + 1))], small)
+
+    @pl.when(is_second)
+    def _():
+        landed(ranks.at[pl.ds(0, mates + 1 + 2 * (NZ - 2 - NEAR))], small)
+
+    @pl.when(is_end)
+    def _():
+        landed(ranks.at[pl.ds(0, mates + 1)], small)
 
     @pl.when(jnp.logical_not(edge_plane))
     def _():
         mine_to_root.wait_send()
-
-    @pl.when(is_root)
-    def _():
-        landed(late.at[pl.ds(0, mates)], l_ss)
-        for copy in passed:
-            copy.wait_send()
-
-    @pl.when(is_caster)
-    def _():
-        landed(ranks, b_ss)
 
 
 def body(block_cols, step_tiles, mass, warm_start, source_ids):
@@ -385,7 +381,7 @@
         out_specs=pl.BlockSpec(memory_space=pltpu.VMEM),
         scratch_shapes=[
             pltpu.SMEM(block_cols.shape, jnp.int32),
-            pltpu.VMEM(step_tiles.shape, F32),
+            pltpu.VMEM((6, tile, tile), F32),
             pltpu.VMEM(mass.shape, F32),
             pltpu.VMEM((rows, width), F32),
             pltpu.VMEM(source_ids.shape, jnp.int32),
@@ -394,24 +390,19 @@
             pltpu.VMEM(edge, F32), pltpu.VMEM(edge[1:], F32),
             pltpu.VMEM(square, F32), pltpu.VMEM(edge[1:], F32),
             pltpu.VMEM(sums, F32),
-            pltpu.VMEM((2 * NZ - 2, *sums), F32),
+            pltpu.VMEM((2 * NZ - 4, *sums), F32),
             pltpu.VMEM(sums, F32),
             pltpu.VMEM((5 * nx, *sums), F32),
             pltpu.VMEM(sums, F32),
             sem((5,)),
-            sem((2,)), sem((3,)),
-            sem((2,)), sem((3,)),
+            sem((3,)), sem((3,)),
             sem, sem,
-            sem, sem,
-            sem, sem,
-            sem((2,)), pltpu.SemaphoreType.REGULAR,
-            sem, sem,
-            sem, sem,
-            sem, sem,
+            pltpu.SemaphoreType.REGULAR,
+            sem,
         ],
         compiler_params=pltpu.CompilerParams(collective_id=0, has_side_effects=True),
         name="heat",
-    )(block_cols, step_tiles, mass, warm_start, source_ids)
+    )(block_cols, step_tiles.reshape(6, tile, tile), mass, warm_start, source_ids)
 
 
 def solution(mesh):

time: 59.6 us -> 58.5 us (0.982)
  Pallas kernels: 58.8 us -> 57.7 us
    pallas_call x1, Pallas kernels: 58.8 us -> 57.7 us  [body(): pl.pallas_call(functools.partial(kernel, nx, tile), out_shape=pltpu.VMEM(...]
where the time goes in v5:
time: 58.5 us; the launch traced here: 58.4 us
  Pallas kernels  57.7 us (99%)
  local copies, waits for them, and re-layouts  0.66 us (1%)
    pallas_call x1, Pallas kernels, body(): pl.pallas_call(functools.partial(kernel, nx, tile), out_shape=pltpu.VMEM(...  57.7 us

profile of v5, /device:TPU:40, one launch (start us, length us, event | category | flops | bytes accessed | tf_op | source)
XLA Modules:
  0.0 58.4 jit_solution(8113085812366532571)
XLA Ops:
  0.0 57.7 %heat.1 = f32[256,128]{1,0:T(8,128)S(1)} custom-call(s32[2,3]{1,0:T(2,128)} %cols_h.1, f32[6,128,128]{2,1,0:T(8,128)} %bitcast.1, f32[256]{0:T(256)} %mass_h.1, f32[256,128]{1,0:T(8,128)} %x_h.1, s32[128]{0:T(128)} %src_h.1), custom_call_target="tpu_custom_call" | custom-call | tf_op jit(solution)/shard_map/heat/pallas_call | solution.py:377
  57.7 0.7 %copy.7 = f32[256,128]{1,0:T(8,128)} copy(f32[256,128]{1,0:T(8,128)S(1)} %heat.1) | data formatting | bytes 262144

commit v6 on v5

--- a/solution.py
+++ b/solution.py
@@ -298,9 +298,9 @@
         late[slot] = mine
         landed(late.at[pl.ds(0, count - 1)], l_rs)
 
-    def to_chip_at(k):
+    def to_chip_at(k, x_at=px):
         return [
-            pltpu.make_async_remote_copy(total, total, small, l_rs, device_id=(g, px, k, c), device_id_type=MESH)
+            pltpu.make_async_remote_copy(total, total, small, l_rs, device_id=(g, x_at, k, c), device_id_type=MESH)
             for c in (1, 0)
         ]
 
@@ -320,11 +320,12 @@
         landed(total, l_rs)
 
     is_second = last & (pc == 0)
-
-    @pl.when(is_caster)
+    serves, is_server = is_caster & (px > 0), is_root & (px == nx - 1)
+
+    @pl.when(serves | is_server)
     def _():
         for k in (*range(1, NEAR + 1), NZ - 1):
-            for copy in to_chip_at(k):
+            for copy in to_chip_at(k, jnp.where(is_server, 0, px)):
                 copy.start()
 
     @pl.when(is_second)
@@ -349,9 +350,20 @@
     @pl.when(is_root)
     def _():
         landed(halo_x.at[pl.ds(0, 2)], passing)
+
+    @pl.when(is_root & (px < nx - 1))
+    def _():
         landed(ranks.at[pl.ds(0, 2 * mates)], small)
 
-    @pl.when(is_caster)
+    @pl.when(is_server)
+    def _():
+        landed(ranks.at[pl.ds(0, 2 * mates + 2 * (NEAR + 1))], small)
+
+    @pl.when(is_caster & (px == 0))
+    def _():
+        landed(ranks.at[pl.ds(0, mates)], small)
+
+    @pl.when(serves)
     def _():
         landed(ranks.at[pl.ds(0, mates + 2 * (NEAR + 1))], small)
 

time: 58.5 us -> 57.9 us (0.990); the launches traced: 58.4 us -> 56.8 us
  Pallas kernels: 57.7 us -> 56.2 us
    pallas_call x1, Pallas kernels: 57.7 us -> 56.2 us  [body(): pl.pallas_call(functools.partial(kernel, nx, tile), out_shape=pltpu.VMEM(...]
where the time goes in v6:
time: 57.9 us; the launch traced here: 56.8 us
  Pallas kernels  56.2 us (97%)
  local copies, waits for them, and re-layouts  0.66 us (1%)
    pallas_call x1, Pallas kernels, body(): pl.pallas_call(functools.partial(kernel, nx, tile), out_shape=pltpu.VMEM(...  56.2 us

profile of v6, /device:TPU:40, one launch (start us, length us, event | category | flops | bytes accessed | tf_op | source)
XLA Modules:
  0.0 56.8 jit_solution(702937363389128454)
XLA Ops:
  0.0 56.2 %heat.1 = f32[256,128]{1,0:T(8,128)S(1)} custom-call(s32[2,3]{1,0:T(2,128)} %cols_h.1, f32[6,128,128]{2,1,0:T(8,128)} %bitcast.1, f32[256]{0:T(256)} %mass_h.1, f32[256,128]{1,0:T(8,128)} %x_h.1, s32[128]{0:T(128)} %src_h.1), custom_call_target="tpu_custom_call" | custom-call | tf_op jit(solution)/shard_map/heat/pallas_call | solution.py:389
  56.2 0.7 %copy.7 = f32[256,128]{1,0:T(8,128)} copy(f32[256,128]{1,0:T(8,128)S(1)} %heat.1) | data formatting | bytes 262144

commit v7 on v6

--- a/solution.py
+++ b/solution.py
@@ -27,8 +27,8 @@
 
 def product(high, low, packed):
     n = packed.shape[1] // 2
-    both = jnp.dot(high, packed, preferred_element_type=F32) + jnp.dot(low, packed, preferred_element_type=F32)
-    return both[:, :n] + both[:, n:]
+    both = jnp.dot(high, packed, preferred_element_type=F32)
+    return both[:, :n] + (both[:, n:] + jnp.dot(low, packed[:, :n], preferred_element_type=F32))
 
 
 def rows_sum(value):
@@ -52,8 +52,8 @@
     cols_h, tiles_h, mass_h, x_h, src_h,
     out,
     cols, tiles, mass, x, src,
-    halo_x, halo_s, halo_w, halo_m, halo_q, s_buf, w_buf, m_buf, q_buf, own, ranks, line, late, total,
-    in_sem, x_rs, s_rs, mw_rs, qz_rs, up_sem, l_rs,
+    halo_x, halo_s, halo_c, halo_m, halo_q, s_buf, c_buf, m_buf, q_buf, own, ranks, line, late, total,
+    in_sem, x_rs, s_rs, m_rs, q_rs, y_rs, c_rs, z_rs, up_sem, l_rs,
 ):
     large, small, passing = in_sem.at[0], in_sem.at[1], in_sem.at[2]
     g, px, pz, pc = (lax.axis_index(name) for name in AXES)
@@ -90,6 +90,10 @@
     def _():
         greet(*far[1:])
 
+    @pl.when((pc == 1) & jnp.logical_not(first))
+    def _():
+        greet(px, pz - 1, 1)
+
     @pl.when(first)
     def _():
         for d in range(nx):
@@ -109,7 +113,7 @@
 
     mates = 2 * nx - 1
     pl.semaphore_wait(
-        bar, jnp.where(first, mates + jnp.where(is_root, 1, 0), jnp.where(last, 2 + 2 * nx, 3))
+        bar, jnp.where(first, mates + 2 * pc, jnp.where(last, 2 + 2 * nx, 3 + pc))
     )
 
     def send(src, dst, ss, rs, to):
@@ -153,6 +157,7 @@
     inner = halves(jnp.concatenate([jnp.concatenate([t00, t01], axis=1), jnp.concatenate([t10, t11], axis=1)], axis=0))
     to_left, to_right = halves(t0l), halves(t1r)
 
+    ceiling = 2.0 * jnp.max(diag, axis=0, keepdims=True)
     x_pair = pair(x[...])
     ids = lax.broadcasted_iota(jnp.int32, (2 * tile, src.shape[0]), 0) + position * 2 * tile
     rhs = (ids == src[...].reshape(1, -1)).astype(F32)
@@ -164,8 +169,14 @@
     send(s_buf.at[0], halo_s.at[way_slot], large, s_rs.at[way_slot], by_way)
     send(s_buf.at[1], halo_s.at[0], large, s_rs.at[0], right)
     to_chip = [
-        pltpu.make_async_remote_copy(m_buf, halo_m, large, mw_rs, device_id=right, device_id_type=MESH),
-        pltpu.make_async_remote_copy(q_buf, halo_q, large, qz_rs, device_id=right, device_id_type=MESH),
+        pltpu.make_async_remote_copy(src, dst, large, rs, device_id=(*right[:3], 1), device_id_type=MESH)
+        for src, dst, rs in ((m_buf, halo_m, m_rs), (q_buf, halo_q, q_rs))
+    ]
+    to_core = [
+        pltpu.make_async_remote_copy(
+            c_buf.at[i], halo_c.at[i], passing, y_rs if i == 4 else c_rs, device_id=partner, device_id_type=MESH
+        )
+        for i in range(5)
     ]
 
     passed = [
@@ -197,6 +208,8 @@
 
     @pl.when(pc == 0)
     def _():
+        c_buf[4] = on_left
+        to_core[4].start()
         landed(halo_x.at[0], x_rs.at[0])
 
     landed(halo_x.at[1], x_rs.at[1])
@@ -208,44 +221,50 @@
     landed(halo_s.at[1], s_rs.at[1])
     next_r = [halo_s[0] + on_left, halo_s[1] + on_right]
     w = near_r - jnp.concatenate([product(*to_left, pair(next_r[0])), product(*to_right, pair(next_r[1]))], axis=0)
-    to_core = pltpu.make_async_remote_copy(
-        w_buf, halo_w, large, mw_rs, device_id=partner, device_id_type=MESH
-    )
 
     @pl.when(pc == 0)
     def _():
-        w_buf[...] = w[tile:]
-        to_core.start()
-
+        for i, value in enumerate((w[tile:], back_r, next_r[0])):
+            c_buf[i] = value
+            to_core[i].start()
 
     w_pair = pair(w)
     sq, cross = rows_sum(r * r), rows_sum(r * w)
-    ceiling = 2.0 * jnp.max(diag)
     about = jnp.where(sq > 0, jnp.clip(cross / sq, 0.0, ceiling), 0.0)
     u = w - about * r
     rss = rows_sum(u * u)
     near_u = diag * w - product(*inner, w_pair) - about * near_r
-    back_u = product(*from_left, w_pair[:tile]) - about * back_r
+    back_w = product(*from_left, w_pair[:tile])
+
+    @pl.when(pc == 0)
+    def _():
+        c_buf[3] = back_w
+        to_core[3].start()
+
     quad, lin, curv = rows_sum(u * near_u), 2.0 * rows_sum(r * near_u), rows_sum(r * near_r)
 
-    @pl.when(pc == 0)
-    def _():
-        landed(halo_m, mw_rs)
-        across_m = product(*halves(halo_m[...]), pair(on_left)) - back_r
-        landed(halo_q, qz_rs)
-        halo_w[...] = halo_q[...] + across_m
+    own[...] = jnp.concatenate([sq, cross, about, rss, quad, lin, curv, jnp.zeros_like(sq)], axis=0)
 
     @pl.when(pc == 1)
     def _():
-        landed(halo_w, mw_rs)
-
-    next_u = halo_w[...] - about * next_r[0]
-    quad -= 2.0 * rows_sum(back_u * next_u)
-    lin -= 2.0 * rows_sum(back_u * next_r[0] + back_r * next_u)
-    curv -= 2.0 * rows_sum(back_r * next_r[0])
+        landed(halo_c.at[4], y_rs)
+        landed(halo_m, m_rs)
+        across_m = product(*halves(halo_m[...]), pair(halo_c[4]))
+        landed(halo_q, q_rs)
+        landed(halo_c.at[pl.ds(0, 4)], c_rs)
+        w_at, back_r_at, next_r_at, back_w_at = (halo_c[i] for i in range(4))
+        quads, lins, curvs = quad, lin, curv
+        for edge_w, edge_r, edge_back_w, edge_back_r in (
+            (w_at, next_r[0], back_w, back_r),
+            (halo_q[...] + across_m - back_r_at, next_r_at, back_w_at, back_r_at),
+        ):
+            edge_u, edge_back_u = edge_w - about * edge_r, edge_back_w - about * edge_back_r
+            quads -= 2.0 * rows_sum(edge_back_u * edge_u)
+            lins -= 2.0 * rows_sum(edge_back_u * edge_r + edge_back_r * edge_u)
+            curvs -= 2.0 * rows_sum(edge_back_r * edge_r)
+        own[pl.ds(4, 3), :] = jnp.concatenate([quads, lins, curvs], axis=0)
+
     blank = jnp.zeros((1, sq.shape[1]), F32)
-    mine = jnp.concatenate([sq, cross, about, rss, quad, lin, curv, blank], axis=0)
-    own[...] = mine
 
     edge_plane = first | last
     slot = jnp.where(edge_plane, nx + jnp.where(first, 2 * nx, 0) + px * 2 + pc, 0)
@@ -263,7 +282,7 @@
     mine_out, line_out = share(own, slot, others), share(line, px, others)
     (mine_down,) = share(own, slot, [(0, 0)])
     mine_to_root = pltpu.make_async_remote_copy(
-        own, ranks.at[rank], small, qz_rs, device_id=(g, px, 0, 1), device_id_type=MESH
+        own, ranks.at[rank], small, z_rs, device_id=(g, px, 0, 1), device_id_type=MESH
     )
 
     @pl.when(edge_plane)
@@ -284,18 +303,18 @@
     @pl.when(is_root)
     def _():
         inner_planes = ranks.at[pl.ds(0, 2 * NZ - 4)]
-        landed(inner_planes, qz_rs)
+        landed(inner_planes, z_rs)
         joined = jnp.concatenate([*merged(inner_planes), blank], axis=0)
         line[...] = joined
         for copy in line_out:
             copy.start()
         late[px] = joined
-        late[slot] = mine
+        late[slot] = own[...]
         landed(late.at[pl.ds(0, count - 2)], l_rs)
 
     @pl.when(is_caster)
     def _():
-        late[slot] = mine
+        late[slot] = own[...]
         landed(late.at[pl.ds(0, count - 1)], l_rs)
 
     def to_chip_at(k, x_at=px):
@@ -341,7 +360,8 @@
 
     @pl.when(pc == 0)
     def _():
-        landed(tiles.at[pl.ds(0, 5)], large)
+        landed(tiles.at[pl.ds(0, 4)], large)
+        landed(tiles.at[pl.ds(0, 5)], passing)
 
     @pl.when(pc == 1)
     def _():
@@ -397,9 +417,9 @@
             pltpu.VMEM(mass.shape, F32),
             pltpu.VMEM((rows, width), F32),
             pltpu.VMEM(source_ids.shape, jnp.int32),
-            pltpu.VMEM(slots, F32), pltpu.VMEM(slots, F32), pltpu.VMEM(edge[1:], F32),
+            pltpu.VMEM(slots, F32), pltpu.VMEM(slots, F32), pltpu.VMEM((5, *edge[1:]), F32),
             pltpu.VMEM(square, F32), pltpu.VMEM(edge[1:], F32),
-            pltpu.VMEM(edge, F32), pltpu.VMEM(edge[1:], F32),
+            pltpu.VMEM(edge, F32), pltpu.VMEM((5, *edge[1:]), F32),
             pltpu.VMEM(square, F32), pltpu.VMEM(edge[1:], F32),
             pltpu.VMEM(sums, F32),
             pltpu.VMEM((2 * NZ - 4, *sums), F32),
@@ -408,7 +428,7 @@
             pltpu.VMEM(sums, F32),
             sem((5,)),
             sem((3,)), sem((3,)),
-            sem, sem,
+            sem, sem, sem, sem, sem,
             pltpu.SemaphoreType.REGULAR,
             sem,
         ],

time: 57.9 us -> 57.9 us (level)
  no operation moved by 1% of the time
where the time goes in v7:
time: 57.9 us; the launch traced here: 56.8 us
  Pallas kernels  56.1 us (97%)
  local copies, waits for them, and re-layouts  0.66 us (1%)
    pallas_call x1, Pallas kernels, body(): pl.pallas_call(functools.partial(kernel, nx, tile), out_shape=pltpu.VMEM(...  56.1 us

profile of v7, /device:TPU:40, one launch (start us, length us, event | category | flops | bytes accessed | tf_op | source)
XLA Modules:
  0.0 56.8 jit_solution(8915299357442329259)
XLA Ops:
  0.0 56.1 %heat.1 = f32[256,128]{1,0:T(8,128)S(1)} custom-call(s32[2,3]{1,0:T(2,128)} %cols_h.1, f32[6,128,128]{2,1,0:T(8,128)} %bitcast.1, f32[256]{0:T(256)} %mass_h.1, f32[256,128]{1,0:T(8,128)} %x_h.1, s32[128]{0:T(128)} %src_h.1), custom_call_target="tpu_custom_call" | custom-call | tf_op jit(solution)/shard_map/heat/pallas_call | solution.py:409
  56.1 0.7 %copy.7 = f32[256,128]{1,0:T(8,128)} copy(f32[256,128]{1,0:T(8,128)S(1)} %heat.1) | data formatting | bytes 262144

commit v8 on v7

--- a/solution.py
+++ b/solution.py
@@ -262,7 +262,7 @@
             quads -= 2.0 * rows_sum(edge_back_u * edge_u)
             lins -= 2.0 * rows_sum(edge_back_u * edge_r + edge_back_r * edge_u)
             curvs -= 2.0 * rows_sum(edge_back_r * edge_r)
-        own[pl.ds(4, 3), :] = jnp.concatenate([quads, lins, curvs], axis=0)
+        own[...] = jnp.concatenate([sq, cross, about, rss, quads, lins, curvs, jnp.zeros_like(sq)], axis=0)
 
     blank = jnp.zeros((1, sq.shape[1]), F32)
 
@@ -325,7 +325,7 @@
 
     @pl.when(first)
     def _():
-        sq, cross, _, rss, quad, _, _ = merged(late)
+        sq, cross, _, rss, quad, _, _ = merged(late.at[pl.ds(0, count)])
         step = sq / cross
         after = step * step * rss
         ratio = after / sq
@@ -422,9 +422,9 @@
             pltpu.VMEM(edge, F32), pltpu.VMEM((5, *edge[1:]), F32),
             pltpu.VMEM(square, F32), pltpu.VMEM(edge[1:], F32),
             pltpu.VMEM(sums, F32),
-            pltpu.VMEM((2 * NZ - 4, *sums), F32),
+            pltpu.VMEM((2 * NZ, *sums), F32),
             pltpu.VMEM(sums, F32),
-            pltpu.VMEM((5 * nx, *sums), F32),
+            pltpu.VMEM((6 * nx, *sums), F32),
             pltpu.VMEM(sums, F32),
             sem((5,)),
             sem((3,)), sem((3,)),

time: 57.9 us -> 57.9 us (level)
  no operation moved by 1% of the time
where the time goes in v8:
time: 57.9 us; the launch traced here: 56.8 us
  Pallas kernels  56.1 us (97%)
  local copies, waits for them, and re-layouts  0.66 us (1%)
    pallas_call x1, Pallas kernels, body(): pl.pallas_call(functools.partial(kernel, nx, tile), out_shape=pltpu.VMEM(...  56.1 us

profile of v8, /device:TPU:40, one launch (start us, length us, event | category | flops | bytes accessed | tf_op | source)
XLA Modules:
  0.0 56.8 jit_solution(2894284767201084469)
XLA Ops:
  0.0 56.1 %heat.1 = f32[256,128]{1,0:T(8,128)S(1)} custom-call(s32[2,3]{1,0:T(2,128)} %cols_h.1, f32[6,128,128]{2,1,0:T(8,128)} %bitcast.1, f32[256]{0:T(256)} %mass_h.1, f32[256,128]{1,0:T(8,128)} %x_h.1, s32[128]{0:T(128)} %src_h.1), custom_call_target="tpu_custom_call" | custom-call | tf_op jit(solution)/shard_map/heat/pallas_call | solution.py:409
  56.1 0.7 %copy.7 = f32[256,128]{1,0:T(8,128)} copy(f32[256,128]{1,0:T(8,128)S(1)} %heat.1) | data formatting | bytes 262144
